TPU v7x, 32 devices: a whole 2x2x4 slice. The times are simulated.
32 devices in a mesh: layer: 2 (over x), col: 4 (over z), row: 4 (over y, core).
Axes of the slice: x: 2, y: 2, z: 4, core: 2. Of those that a mesh axis runs over, the one named last changes fastest.
Arguments:
- weight: float32 [2048, 4096], P(('layer', 'row'), 'col'), parts along dimension 0
- grad_in: float32 [2048, 4096], P(('layer', 'row'), 'col'), parts along dimension 0
- mom_first: float32 [2048, 4096], P(('layer', 'row'), 'col'), parts along dimension 0
- mom_second: float32 [2048, 4096], P(('layer', 'row'), 'col'), parts along dimension 0
- stat_left: float32 [2048, 1024], P(('layer', 'row'), 'col'), parts along dimension 0
- stat_right: float32 [8192, 4096], P(('layer', 'row'), 'col'), parts along dimension 0
- basis_left: float32 [2048, 1024], P(('layer', 'row'), 'col'), parts along dimension 0
- basis_right: float32 [8192, 4096], P(('layer', 'row'), 'col'), parts along dimension 0
Outputs:
- output 1: float32 [2048, 4096], P(('layer', 'row'), 'col'), parts along dimension 0
- output 2: float32 [2048, 4096], P(('layer', 'row'), 'col'), parts along dimension 0
- output 3: float32 [2048, 4096], P(('layer', 'row'), 'col'), parts along dimension 0
- output 4: float32 [2048, 1024], P(('layer', 'row'), 'col'), parts along dimension 0
- output 5: float32 [8192, 4096], P(('layer', 'row'), 'col'), parts along dimension 0
There are 2 independent parts. A program takes and returns all parts, laid end to end along the dimension named above; each array names one.
All inputs are finite; a program needn't handle non-finite values.
Results may differ from a plain program's by a relative error of at most 0.001.
Values are sent between devices in bfloat16 or wider.
A program may use at most 1 GiB of HBM per device.

v0:
```python
import jax
import jax.numpy as jnp
from jax import lax
from jax.sharding import PartitionSpec as P

BETA1 = 0.9
BETA2 = 0.9
EPS = 1e-8
LR = 0.1
STEP = 10
BIAS_ONE = 1.0 - BETA1 ** STEP
BIAS_TWO = 1.0 - BETA2 ** STEP


def solution(mesh):
    tile_spec = P(("layer", "row"), "col")
    highest = lax.Precision.HIGHEST
    contract_rows = (((0,), (0,)), ((), ()))
    contract_cols = (((1,), (1,)), ((), ()))

    def local_step(weight, grad_in, mom_first, mom_second, stat_left, stat_right, basis_left, basis_right):
        grad_rows = lax.all_gather(grad_in, "col", axis=1, tiled=True)
        grad_cols = lax.all_gather(grad_in, "row", axis=0, tiled=True)
        left_part = lax.dot_general(grad_in, grad_cols, contract_cols, precision=highest, preferred_element_type=jnp.float32)
        left_sum = lax.psum_scatter(left_part, "col", scatter_dimension=1, tiled=True)
        right_part = lax.dot_general(grad_rows, grad_in, contract_rows, precision=highest, preferred_element_type=jnp.float32)
        right_sum = lax.psum_scatter(right_part, "row", scatter_dimension=0, tiled=True)
        new_left = BETA2 * stat_left + (1.0 - BETA2) * left_sum
        new_right = BETA2 * stat_right + (1.0 - BETA2) * right_sum
        left_rows = lax.all_gather(basis_left.astype(jnp.bfloat16), "col", axis=1, tiled=True)
        right_cols = lax.all_gather(basis_right.astype(jnp.bfloat16), "row", axis=0, tiled=True)
        inner_rot = jnp.dot(grad_rows.astype(jnp.bfloat16), right_cols, preferred_element_type=jnp.float32).astype(jnp.bfloat16)
        rotated_part = lax.dot_general(left_rows, inner_rot, contract_rows, preferred_element_type=jnp.float32)
        rotated = lax.psum_scatter(rotated_part, "row", scatter_dimension=0, tiled=True)
        new_first = BETA1 * mom_first + (1.0 - BETA1) * rotated
        new_second = BETA2 * mom_second + (1.0 - BETA2) * rotated * rotated
        direction = (new_first / BIAS_ONE) / (jnp.sqrt(new_second / BIAS_TWO) + EPS)
        direction_cols = lax.all_gather(direction.astype(jnp.bfloat16), "row", axis=0, tiled=True)
        back_inner = jnp.dot(left_rows, direction_cols, preferred_element_type=jnp.float32).astype(jnp.bfloat16)
        update_part = lax.dot_general(back_inner, right_cols, contract_cols, preferred_element_type=jnp.float32)
        step_update = lax.psum_scatter(update_part, "col", scatter_dimension=1, tiled=True)
        new_weight = weight - LR * step_update
        return new_weight, new_first, new_second, new_left, new_right

    return jax.shard_map(local_step, mesh=mesh, in_specs=(tile_spec,) * 8, out_specs=(tile_spec,) * 5, check_vma=False)
```

profile of v0, /device:TPU:0, one launch (start us, length us, event | category | flops | bytes accessed | tf_op | source)
XLA Modules:
  0.0 519.6 jit_solution(14317962978673443819)
XLA Ops:
  7.2 0.7 all-gather.5.cloned.1.call-update
  8.0 3.9 convert_element_type.20
  11.9 0.0 reduce-scatter.5.cloned.1.call-start
  11.9 22.5 %all_gather.17 = bf16[256,1024]{1,0:T(8,128)(2,1)S(1)} all-gather(bf16[256,256]{1,0:T(8,128)(2,1)S(1)} %convert_element_type.22), channel_id=1, replica_groups=mesh['layer'=2,'col'=4,'row'=4] {'col'}, dimensions={1}, use_global_device_ids=true | all-gather | bytes 655360 | tf_op jit(solution)/shard_map/all_gather | solution.py:30
  34.4 61.6 %all-gather.5.cloned.1.call-done = f32[256,4096]{1,0:T(8,128)} async-done(((f32[256,1024]{1,0:T(8,128)}), f32[256,4096]{1,0:T(8,128)}) %all-gather.5.cloned.1.call-update) | async-done | bytes 4194320 | tf_op jit(solution)/shard_map/all_gather | solution.py:22
  96.0 60.4 %all-gather.7.cloned.1.call-done = bf16[4096,1024]{1,0:T(8,128)(2,1)} async-done(((bf16[1024,1024]{1,0:T(8,128)(2,1)}), bf16[4096,1024]{1,0:T(8,128)(2,1)}) %all-gather.7.cloned.1.call-update) | async-done | bytes 8388624 | tf_op jit(solution)/shard_map/all_gather | solution.py:31
  156.4 9.6 %convolution_bitcast_fusion = f32[1024,1024]{0,1:T(8,128)} fusion(bf16[256,1024]{1,0:T(8,128)(2,1)S(1)} %all_gather.17, bf16[4096,1024]{1,0:T(8,128)(2,1)} %all-gather.7.cloned.1.call-done, f32[256,4096]{1,0:T(8,128)} %all-gather.5.cloned.1.call-done), kind=kOutput, calls=%fused_computation.1 | convolution fusion | flops 2685665280 | bytes 17301504 | tf_op jit(solution)/shard_map/dot_general | solution.py:33
  166.0 0.0 all-gather.11.cloned.1.call-start
  166.0 0.5 all-gather.11.cloned.1.call-update
  166.6 0.6 copy-done.1
  167.2 1.3 copy.13
  168.5 1.3 copy.14
  169.8 40.2 %reduce-scatter.5.cloned.1.call-done = f32[256,1024]{0,1:T(8,128)} async-done(((f32[1024,1024]{0,1:T(8,128)}), f32[256,1024]{0,1:T(8,128)}) %reduce-scatter.5.cloned.1.call-update) | async-done | bytes 1048592 | tf_op jit(solution)/shard_map/reduce_scatter | solution.py:34
  210.0 3.4 divide_convert_fusion
  213.4 0.0 reduce-scatter.9.cloned.1.call-start
  213.4 32.3 %all-gather.11.cloned.1.call-done = f32[1024,1024]{1,0:T(8,128)} async-done(((f32[256,1024]{1,0:T(8,128)}), f32[1024,1024]{1,0:T(8,128)}) %all-gather.11.cloned.1.call-update) | async-done | bytes 4194320 | tf_op jit(solution)/shard_map/all_gather | solution.py:23
  245.7 6.8 %fusion.10 = f32[256,1024]{1,0:T(8,128)} fusion(f32[256,1024]{1,0:T(8,128)S(1)} %copy-done, f32[1024,1024]{1,0:T(8,128)} %all-gather.11.cloned.1.call-done), kind=kOutput, calls=%fused_computation.13 | convolution fusion | flops 3221225472 | bytes 6291456 | tf_op jit(solution)/shard_map/dot_general | solution.py:24
  252.6 0.0 reduce-scatter.7.cloned.1.call-start
  252.6 17.6 %all-gather.9.cloned.1.call-done = bf16[1024,1024]{0,1:T(8,128)(2,1)} async-done(((bf16[256,1024]{0,1:T(8,128)(2,1)}), bf16[1024,1024]{0,1:T(8,128)(2,1)}) %all-gather.9.cloned.1.call-update) | async-done | bytes 2097168 | tf_op jit(solution)/shard_map/all_gather | solution.py:38
  270.3 10.1 %fusion.8 = f32[256,4096]{0,1:T(8,128)} fusion(bf16[4096,1024]{1,0:T(8,128)(2,1)} %all-gather.7.cloned.1.call-done, bf16[1024,1024]{0,1:T(8,128)(2,1)} %all-gather.9.cloned.1.call-done, bf16[256,1024]{1,0:T(8,128)(2,1)} %copy-done.3), kind=kOutput, calls=%fused_computation.11 | convolution fusion | flops 2684616704 | bytes 15204352 | tf_op jit(solution)/shard_map/dot_general | solution.py:40
  280.4 0.2 reduce-scatter.11.cloned.1.call-start
  280.6 17.2 %fusion.11 = f32[4096,1024]{1,0:T(8,128)} fusion(f32[256,4096]{1,0:T(8,128)} %all-gather.5.cloned.1.call-done, f32[256,1024]{1,0:T(8,128)S(1)} %copy-done), kind=kOutput, calls=%fused_computation.14 | convolution fusion | flops 12884901888 | bytes 22020096 | tf_op jit(solution)/shard_map/dot_general | solution.py:26
  297.8 1.6 copy.16
  299.4 0.9 reduce-scatter.9.cloned.1.call-done
  300.3 1.7 multiply_add_fusion.2
  302.0 1.3 copy.18
  303.3 1.3 copy.19
  304.6 73.7 %reduce-scatter.7.cloned.1.call-done = f32[256,1024]{0,1:T(8,128)} async-done(((f32[256,4096]{0,1:T(8,128)}), f32[256,1024]{0,1:T(8,128)}) %reduce-scatter.7.cloned.1.call-update) | async-done | bytes 1048592 | tf_op jit(solution)/shard_map/reduce_scatter | solution.py:41
  378.4 1.4 multiply_subtract_fusion
  379.7 1.3 copy.17
  381.0 124.8 %reduce-scatter.11.cloned.1.call-done = f32[1024,1024]{1,0:T(8,128)} async-done(((f32[4096,1024]{1,0:T(8,128)}), f32[1024,1024]{1,0:T(8,128)}) %reduce-scatter.11.cloned.1.call-update) | async-done | bytes 4194320 | tf_op jit(solution)/shard_map/reduce_scatter | solution.py:27
  505.8 7.0 %multiply_add_fusion = f32[1024,1024]{1,0:T(8,128)} fusion(f32[1024,1024]{1,0:T(8,128)} %reduce-scatter.11.cloned.1.call-done, f32[1024,1024]{1,0:T(8,128)} %param.13), kind=kLoop, calls=%fused_computation | loop fusion | flops 3145728 | bytes 12582912 | tf_op jit(solution)/shard_map/add | solution.py:29
  (21 shorter events, 0.2 us)
Async XLA Ops:
  7.2 88.8 %all-gather.5.cloned.1.call-start = ((), (), s32[]{:S(2)}) async-start(), calls=%async_computation.4 | async-start | bytes 5242880 | tf_op jit(solution)/shard_map/all_gather | solution.py:22
  7.9 4.0 copy-start.5
  7.9 148.5 %all-gather.7.cloned.1.call-start = ((), (), s32[]{:S(2)}) async-start(), calls=%async_computation.5 | async-start | bytes 10485760 | tf_op jit(solution)/shard_map/all_gather | solution.py:31
  11.9 198.1 %reduce-scatter.5.cloned.1.call-start = ((), (), s32[]{:S(2)}) async-start(), calls=%async_computation.6 | async-start | bytes 5242880 | tf_op jit(solution)/shard_map/reduce_scatter | solution.py:34
  34.4 122.0 %copy-start.3 = (bf16[256,1024]{1,0:T(8,128)(2,1)}, bf16[256,1024]{1,0:T(8,128)(2,1)S(1)}, u32[]{:S(2)}) copy-start(bf16[256,1024]{1,0:T(8,128)(2,1)S(1)} %all_gather.17) | copy-start | bytes 1572868
  166.0 1.2 copy-start.1
  166.0 2.5 copy-start.2
  166.0 79.7 %all-gather.11.cloned.1.call-start = ((), (), s32[]{:S(2)}) async-start(), calls=%async_computation.9 | async-start | bytes 5242880 | tf_op jit(solution)/shard_map/all_gather | solution.py:23
  166.6 103.7 %all-gather.9.cloned.1.call-start = ((), (), s32[]{:S(2)}) async-start(), calls=%async_computation.7 | async-start | bytes 2621440 | tf_op jit(solution)/shard_map/all_gather | solution.py:38
  168.5 77.2 %copy-start = (f32[256,1024]{1,0:T(8,128)S(1)}, f32[256,1024]{1,0:T(8,128)}, u32[]{:S(2)}) copy-start(f32[256,1024]{1,0:T(8,128)} %param.9) | copy-start | bytes 3145732
  213.4 87.0 %reduce-scatter.9.cloned.1.call-start = ((), (), s32[]{:S(2)}) async-start(), calls=%async_computation.10 | async-start | bytes 1310720 | tf_op jit(solution)/shard_map/reduce_scatter | solution.py:25
  252.6 125.8 %reduce-scatter.7.cloned.1.call-start = ((), (), s32[]{:S(2)}) async-start(), calls=%async_computation.8 | async-start | bytes 5242880 | tf_op jit(solution)/shard_map/reduce_scatter | solution.py:41
  280.4 225.5 %reduce-scatter.11.cloned.1.call-start = ((), (), s32[]{:S(2)}) async-start(), calls=%async_computation.11 | async-start | bytes 20971520 | tf_op jit(solution)/shard_map/reduce_scatter | solution.py:27
  297.8 2.6 copy-start.4
Sparse Core Ops, SparseCore 0:
  9.5 86.3 all-gather.4
  98.1 58.2 all-gather.6
  166.1 43.8 reduce-scatter.4
  211.4 34.2 all-gather.10
  247.7 22.5 all-gather.8
  273.0 27.2 reduce-scatter.8
  303.2 75.1 reduce-scatter.6
  381.0 124.8 reduce-scatter.10
where the time goes:
time: 520 us
  waiting for transfers between devices  413 us (79%)
  matrix products  43.7 us (8%)
  blocking collectives  22.5 us (4%)
  other arithmetic  17.3 us (3%)
  between operations  14.2 us (3%)
  local copies, waits for them, and re-layouts  8.72 us (2%)
    reduce_scatter x1, waiting for transfers between devices, local_step(): lax.psum_scatter(right_part, 'row', scatter_dimension=0, tiled=True)  125 us
    reduce_scatter x1, waiting for transfers between devices, local_step(): lax.psum_scatter(update_part, 'col', scatter_dimension=1, tiled=True)  73.7 us
    all_gather x1, waiting for transfers between devices, local_step(): grad_rows = lax.all_gather(grad_in, 'col', axis=1, tiled=True)  61.6 us
    all_gather x1, waiting for transfers between devices, local_step(): lax.all_gather(basis_right.astype(jnp.bfloat16), 'row', axis=0, tiled=True)  60.4 us
    reduce_scatter x1, waiting for transfers between devices, local_step(): lax.psum_scatter(rotated_part, 'row', scatter_dimension=0, tiled=True)  40.2 us
    all_gather x1, waiting for transfers between devices, local_step(): grad_cols = lax.all_gather(grad_in, 'row', axis=0, tiled=True)  32.3 us
    all_gather x1, blocking collectives, local_step(): lax.all_gather(basis_left.astype(jnp.bfloat16), 'col', axis=1, tiled=True)  22.5 us
    all_gather x1, waiting for transfers between devices, local_step(): lax.all_gather(direction.astype(jnp.bfloat16), 'row', axis=0, tiled=True)  17.6 us
  transfers between devices with their start and end apart: 8, of which 8 were waited for; matrix products, arithmetic and copies ran while one was open for 10% of the time, Pallas kernels for 0%

commit v1 on v0

v1 whole, which is shorter than its diff:
```python
import jax
import jax.numpy as jnp
from jax import lax
from jax.experimental import pallas as pl
from jax.experimental.pallas import tpu as pltpu
from jax.sharding import PartitionSpec as P

BETA1 = 0.9
BETA2 = 0.9
EPS = 1e-8
LR = 0.1
STEP = 10
BIAS_ONE = 1.0 - BETA1 ** STEP
BIAS_TWO = 1.0 - BETA2 ** STEP

MESH = pl.DeviceIdType.MESH
F32 = jnp.float32
BF16 = jnp.bfloat16
NQ = 4
NH = 2
NU = 2
NDEV = 4
NSEND = 160

ROWS_T = (((0,), (0,)), ((), ()))
COLS_T = (((1,), (1,)), ((), ()))


def split3(x):
    a0 = x.astype(BF16)
    r = x - a0.astype(F32)
    a1 = r.astype(BF16)
    a2 = (r - a1.astype(F32)).astype(BF16)
    return a0, a1, a2


def kernel(
    w_hbm, g_hbm, m_hbm, v_hbm, l_hbm, r_hbm, ql_hbm, qr_hbm,
    w_out, m_out, v_out, l_out, r_out,
    grow, gbf, gi, gj, qrc, hcol, ncol, gis, gicat, gjcat, racc, ubuf, urecv,
    wbuf, mbuf, vbuf, qlr, qlc, hacc, kb, qlf, lbuf, lx, lrecv,
    ssem, lsem, r_gbf, r_qlr, r_g32, r_qr, r_qlc, r_h, r_n, r_gj, r_gi, r_u, r_l,
):
    lay = lax.axis_index("layer")
    z = lax.axis_index("col")
    i = lax.axis_index("row")
    y, c = i // 2, i % 2
    sib = 2 * y + (1 - c)
    opp = 2 * (1 - y) + c
    dia = 2 * (1 - y) + (1 - c)
    tr, tc = grow.shape[1], grow.shape[2]
    qrows = tc // NQ
    hcols = tc // NH
    urows = tr // NU

    waits = []
    count = [0]

    def dev(row, col):
        return (lay, col, row)

    def send(src, dst, rsem, row, col, cond=None):
        n = count[0]
        count[0] += 1

        def make():
            return pltpu.make_async_remote_copy(
                src_ref=src(), dst_ref=dst(), send_sem=ssem.at[n], recv_sem=rsem(),
                device_id=dev(row, col), device_id_type=MESH,
            )

        def go():
            make().start()

        def done():
            make().wait_send()

        if cond is None:
            go()
        else:
            pl.when(cond)(go)
        waits.append((cond, done))

    def arrived(dst, rsem, row, col):
        pltpu.make_async_remote_copy(
            src_ref=dst, dst_ref=dst, send_sem=ssem.at[0], recv_sem=rsem,
            device_id=dev(row, col), device_id_type=MESH,
        ).wait_recv()

    loads = {}

    def load(name, n, src, dst):
        cp = pltpu.make_async_copy(src, dst, lsem.at[n])
        cp.start()
        loads[name] = cp

    load("g", 0, g_hbm, grow.at[z])
    for q in range(NQ):
        rows = pl.ds(q * qrows, qrows)
        load(("qr", q), 1 + q, qr_hbm.at[rows], racc.at[rows])
    load("ql", 5, ql_hbm, qlf)
    load("m", 6, m_hbm, mbuf)
    load("v", 7, v_hbm, vbuf)
    load("w", 8, w_hbm, wbuf)
    load("l", 9, l_hbm, lbuf)

    barrier = pltpu.get_barrier_semaphore()
    for row in (sib, opp, dia):
        pl.semaphore_signal(barrier, inc=1, device_id=dev(row, z), device_id_type=MESH)

    @pl.when(z > 0)
    def _():
        pl.semaphore_signal(barrier, inc=1, device_id=dev(i, z - 1), device_id_type=MESH)

    @pl.when(z < NDEV - 1)
    def _():
        pl.semaphore_signal(barrier, inc=1, device_id=dev(i, z + 1), device_id_type=MESH)

    inner = jnp.logical_and(z > 0, z < NDEV - 1)

    @pl.when(inner)
    def _():
        pl.semaphore_wait(barrier, 5)

    @pl.when(jnp.logical_not(inner))
    def _():
        pl.semaphore_wait(barrier, 4)

    def line_own(buf, rs):
        send(lambda: buf.at[z], lambda: buf.at[z], lambda: rs.at[z], i, z + 1, z < NDEV - 1)
        send(lambda: buf.at[z], lambda: buf.at[z], lambda: rs.at[z], i, z - 1, z > 0)

    def line_forward(buf, rs, s):
        right = jnp.logical_and(z >= s, z < NDEV - 1)
        left = jnp.logical_and(z + s < NDEV, z > 0)

        @pl.when(right)
        def _():
            arrived(buf.at[z - s], rs.at[z - s], i, z - 1)

        send(lambda: buf.at[z - s], lambda: buf.at[z - s], lambda: rs.at[z - s], i, z + 1, right)

        @pl.when(left)
        def _():
            arrived(buf.at[z + s], rs.at[z + s], i, z + 1)

        send(lambda: buf.at[z + s], lambda: buf.at[z + s], lambda: rs.at[z + s], i, z - 1, left)

    def line_last(buf, rs, s):
        @pl.when(jnp.logical_and(z >= s, z == NDEV - 1))
        def _():
            arrived(buf.at[z - s], rs.at[z - s], i, z - 1)

        @pl.when(jnp.logical_and(z + s < NDEV, z == 0))
        def _():
            arrived(buf.at[z + s], rs.at[z + s], i, z + 1)

    loads["g"].wait()
    gbf[z] = grow[z].astype(BF16)
    loads["ql"].wait()
    qlr[z] = qlf[...].astype(BF16)

    def qr_own(q):
        rows = pl.ds(q * qrows, qrows)
        for row in (opp, sib):
            send(lambda: qrc.at[i, rows], lambda: qrc.at[i, rows], lambda: r_qr.at[i, q], row, z)

    line_own(gbf, r_gbf)
    for q in range(NQ):
        rows = pl.ds(q * qrows, qrows)
        loads[("qr", q)].wait()
        qrc[i, rows] = racc[rows].astype(BF16)
        if q == 1:
            line_own(qlr, r_qlr)
        if q >= 1:
            qr_own(q - 1)
    load("r", 10, r_hbm, racc)

    def qr_forward(q):
        rows = pl.ds(q * qrows, qrows)
        arrived(qrc.at[opp, rows], r_qr.at[opp, q], opp, z)
        send(lambda: qrc.at[opp, rows], lambda: qrc.at[opp, rows], lambda: r_qr.at[opp, q], sib, z)

    def h_add(k, q, first=False):
        rows = pl.ds(q * qrows, qrows)
        part = jnp.dot(gbf[k, :, rows], qrc[k, rows], preferred_element_type=F32)
        if first:
            hacc[...] = part
        else:
            hacc[...] += part

    qr_own(NQ - 1)

    line_forward(gbf, r_gbf, 1)
    line_forward(qlr, r_qlr, 1)
    qr_forward(0)
    line_forward(gbf, r_gbf, 2)
    line_forward(qlr, r_qlr, 2)
    line_own(grow, r_g32)
    qr_forward(1)
    for s in range(1, NDEV):
        line_last(gbf, r_gbf, s)
        line_last(qlr, r_qlr, s)

    for row in (opp, dia, sib):
        send(lambda row=row: qlr.at[row], lambda: qlc.at[i], lambda: r_qlc.at[i], row, z)
    qlc[i] = qlr[i]

    for q in range(NQ):
        h_add(i, q, first=q == 0)
    for q in range(NQ):
        rows = pl.ds(q * qrows, qrows)
        arrived(qrc.at[sib, rows], r_qr.at[sib, q], sib, z)
        h_add(sib, q)
    qr_forward(2)
    for q in range(2):
        h_add(opp, q)
    for q in range(2):
        rows = pl.ds(q * qrows, qrows)
        arrived(qrc.at[dia, rows], r_qr.at[dia, q], sib, z)
        h_add(dia, q)
    h_add(opp, 2)
    qr_forward(3)
    h_add(opp, 3)
    for q in range(2, NQ):
        rows = pl.ds(q * qrows, qrows)
        arrived(qrc.at[dia, rows], r_qr.at[dia, q], sib, z)
        h_add(dia, q)

    def own_part(buf, rs, n):
        cols = pl.ds(n * hcols, hcols)
        for row in (opp, sib):
            send(lambda: buf.at[i, :, cols], lambda: buf.at[i, :, cols], lambda: rs.at[i, n], row, z)

    def forward_part(buf, rs, n):
        cols = pl.ds(n * hcols, hcols)
        arrived(buf.at[opp, :, cols], rs.at[opp, n], opp, z)
        send(lambda: buf.at[opp, :, cols], lambda: buf.at[opp, :, cols], lambda: rs.at[opp, n], sib, z)

    def rest_part(buf, rs, n):
        cols = pl.ds(n * hcols, hcols)
        arrived(buf.at[sib, :, cols], rs.at[sib, n], sib, z)
        arrived(buf.at[dia, :, cols], rs.at[dia, n], sib, z)

    hcol[i] = hacc[...].astype(BF16)
    for n in range(NH):
        own_part(hcol, r_h, n)

    line_forward(grow, r_g32, 1)
    for row in (opp, dia, sib):
        arrived(qlc.at[row], r_qlc.at[row], row, z)
    loads["m"].wait()
    loads["v"].wait()

    for n in range(NH):
        cols = pl.ds(n * hcols, hcols)
        forward_part(hcol, r_h, n)
        rest_part(hcol, r_h, n)
        rotated = sum(
            lax.dot_general(qlc[k], hcol[k, :, cols], ROWS_T, preferred_element_type=F32) for k in range(NDEV)
        )
        hacc[:, cols] = rotated
        rotated = hacc[:, cols]
        new_first = BETA1 * mbuf[:, cols] + (1.0 - BETA1) * rotated
        new_second = BETA2 * vbuf[:, cols] + (1.0 - BETA2) * rotated * rotated
        mbuf[:, cols] = new_first
        vbuf[:, cols] = new_second
        direction = (new_first / BIAS_ONE) / (jnp.sqrt(new_second / BIAS_TWO) + EPS)
        ncol[i, :, cols] = direction.astype(BF16)
        own_part(ncol, r_n, n)
    stores = []

    def store(n, src, dst):
        cp = pltpu.make_async_copy(src, dst, lsem.at[n])
        cp.start()
        stores.append(cp)

    store(11, mbuf, m_out)
    store(12, vbuf, v_out)

    line_forward(grow, r_g32, 2)
    for row, slot in ((opp, 1), (sib, 0)):
        send(lambda: grow.at[z], lambda slot=slot: gj.at[slot], lambda slot=slot: r_gj.at[slot], row, z)

    def gi_send(b, valid):
        send(lambda: grow.at[b], lambda: gi.at[i], lambda: r_gi.at[i], b, z, jnp.logical_and(valid, b != i))

    gi_send(z, z >= 0)
    line_last(grow, r_g32, 1)
    gi_send(z - 1, z >= 1)
    gi_send(z + 1, z + 1 < NDEV)

    for n in range(NH):
        forward_part(ncol, r_n, n)
        rest_part(ncol, r_n, n)
        cols = pl.ds(n * hcols, hcols)
        kb[:, cols] = sum(
            jnp.dot(qlr[k], ncol[k, :, cols], preferred_element_type=F32) for k in range(NDEV)
        ).astype(BF16)

    def u_send(a, h, slot, col, cond):
        rows = pl.ds(h * urows, urows)
        send(lambda: ubuf.at[a, rows], lambda: urecv.at[slot, rows], lambda: r_u.at[slot, h], i, col, cond)

    for piece in (3, 0, 2, 1):
        ubuf[piece] = lax.dot_general(kb[...], qrc[piece], COLS_T, preferred_element_type=F32)
        for h in range(NU):
            if piece > 0:
                u_send(piece, h, piece, z + 1, z == 0)
            if piece < NDEV - 1:
                u_send(piece, h, NDEV if piece == NDEV - 2 else piece, z - 1, z == NDEV - 1)

    def u_at(a, h, station, to_right):
        rows = pl.ds(h * urows, urows)
        slot = NDEV if (not to_right and station == a) else a

        @pl.when(z == station)
        def _():
            arrived(urecv.at[slot, rows], r_u.at[slot, h], i, station - 1 if to_right else station + 1)
            ubuf[a, rows] += urecv[slot, rows]

        if station != a:
            nxt = station + 1 if to_right else station - 1
            nslot = NDEV if (not to_right and nxt == a) else a
            u_send(a, h, nslot, nxt, z == station)

    line_last(grow, r_g32, 2)
    gi_send(z - 2, z >= 2)
    gi_send(z + 2, z + 2 < NDEV)

    def u_round(t):
        for h in range(NU):
            for a in (3, 2, 1):
                st = t - (3 - a)
                if 1 <= st <= a:
                    u_at(a, h, st, True)
                    u_at(NDEV - 1 - a, h, NDEV - 1 - st, False)

    def to_row():
        gi[i] = grow[i]

    def gj_forward():
        arrived(gj.at[1], r_gj.at[1], opp, z)
        send(lambda: gj.at[1], lambda: gj.at[2], lambda: r_gj.at[2], sib, z)

    def split_gi(k):
        a0, a1, a2 = split3(gi[k])
        gis[k, 0] = a0
        gis[k, 1] = a1
        gis[k, 2] = a2

    mrows = tr

    def right_add(k, gj_ref, first=False):
        b0, b1, b2 = split3(gj_ref[...])
        for n, b in enumerate((b0, b1, b2, b0, b1, b0)):
            gjcat[pl.ds(n * tr, tr)] = b
        a = [gis[k, n].T for n in range(3)]
        for n, t in enumerate((0, 0, 0, 1, 1, 2)):
            gicat[:, pl.ds(n * tr, tr)] = a[t]

        def body(m, carry):
            rows = pl.ds(pl.multiple_of(m * mrows, mrows), mrows)
            part = jnp.dot(gicat[rows], gjcat[...], preferred_element_type=F32)
            old = racc[rows]
            racc[rows] = (BETA2 * old if first else old) + (1.0 - BETA2) * part
            return carry

        lax.fori_loop(0, tc // mrows, body, 0)

    u_round(1)
    line_last(grow, r_g32, 3)
    gi_send(z - 3, z >= 3)
    gi_send(z + 3, z + 3 < NDEV)
    to_row()
    gj_forward()
    loads["r"].wait()
    split_gi(i)
    right_add(i, grow.at[z], first=True)

    def gi_wait(row):
        arrived(gi.at[row], r_gi.at[row], row, z)
        split_gi(row)

    gi_wait(sib)
    arrived(gj.at[0], r_gj.at[0], sib, z)
    right_add(sib, gj.at[0])
    u_round(2)
    gi_wait(opp)
    right_add(opp, gj.at[1])
    gi_wait(dia)

    def left_part(k, n):
        pieces = [gis[k, t] for t in range(3)]
        other = [gis[z, t] for t in range(3)]
        total = None
        for t, u in ((0, 0), (0, 1), (1, 0), (1, 1), (0, 2), (2, 0)):
            d = lax.dot_general(pieces[t], other[u], COLS_T, preferred_element_type=F32)
            total = d if total is None else total + d
        lx[n] = total

    left_part(dia, 3)
    left_part(opp, 2)
    send(lambda: lx.at[3], lambda: lrecv.at[2], lambda: r_l.at[2], dia, z)
    send(lambda: lx.at[2], lambda: lrecv.at[1], lambda: r_l.at[1], opp, z)
    left_part(sib, 1)
    left_part(i, 0)
    send(lambda: lx.at[1], lambda: lrecv.at[0], lambda: r_l.at[0], sib, z)

    arrived(gj.at[2], r_gj.at[2], sib, z)
    right_add(dia, gj.at[2])
    store(13, racc, r_out)
    loads["w"].wait()
    u_round(3)
    wbuf[...] = wbuf[...] - LR * ubuf[z]
    store(14, wbuf, w_out)
    loads["l"].wait()
    arrived(lrecv.at[0], r_l.at[0], sib, z)
    arrived(lrecv.at[1], r_l.at[1], opp, z)
    arrived(lrecv.at[2], r_l.at[2], dia, z)
    left_sum = (lx[0] + lrecv[0]) + (lrecv[1] + lrecv[2])
    lbuf[...] = BETA2 * lbuf[...] + (1.0 - BETA2) * left_sum
    store(15, lbuf, l_out)

    for cond, done in waits:
        if cond is None:
            done()
        else:
            pl.when(cond)(done)
    for cp in stores:
        cp.wait()
    assert count[0] <= NSEND, count[0]


def solution(mesh):
    tile_spec = P(("layer", "row"), "col")

    def local_step(weight, grad_in, mom_first, mom_second, stat_left, stat_right, basis_left, basis_right):
        tr, tc = grad_in.shape
        tl = stat_left.shape[0]
        dma = pltpu.SemaphoreType.DMA
        scratch = [
            pltpu.VMEM((4, tr, tc), F32),
            pltpu.VMEM((4, tr, tc), BF16),
            pltpu.VMEM((4, tr, tc), F32),
            pltpu.VMEM((3, tr, tc), F32),
            pltpu.VMEM((4, tc, tc), BF16),
            pltpu.VMEM((4, tr, tc), BF16),
            pltpu.VMEM((4, tr, tc), BF16),
            pltpu.VMEM((4, 3, tr, tc), BF16),
            pltpu.VMEM((tc, 6 * tr), BF16),
            pltpu.VMEM((6 * tr, tc), BF16),
            pltpu.VMEM((tc, tc), F32),
            pltpu.VMEM((4, tr, tc), F32),
            pltpu.VMEM((5, tr, tc), F32),
            pltpu.VMEM((tr, tc), F32),
            pltpu.VMEM((tr, tc), F32),
            pltpu.VMEM((tr, tc), F32),
            pltpu.VMEM((4, tl, tl), BF16),
            pltpu.VMEM((4, tl, tl), BF16),
            pltpu.VMEM((tr, tc), F32),
            pltpu.VMEM((tr, tc), BF16),
            pltpu.VMEM((tl, tl), F32),
            pltpu.VMEM((tl, tl), F32),
            pltpu.VMEM((4, tl, tl), F32),
            pltpu.VMEM((3, tl, tl), F32),
            dma((NSEND,)),
            dma((16,)),
            dma((4,)), dma((4,)), dma((4,)),
            dma((4, NQ)), dma((4,)),
            dma((4, NH)), dma((4, NH)),
            dma((3,)), dma((4,)),
            dma((5, NU)), dma((3,)),
        ]
        any_spec = pl.BlockSpec(memory_space=pl.ANY)
        outs = [weight, mom_first, mom_second, stat_left, stat_right]
        return pl.pallas_call(
            kernel,
            name="soap_step",
            out_shape=[jax.ShapeDtypeStruct(o.shape, o.dtype) for o in outs],
            in_specs=[any_spec] * 8,
            out_specs=[any_spec] * 5,
            scratch_shapes=scratch,
            compiler_params=pltpu.CompilerParams(
                collective_id=0, has_side_effects=True, vmem_limit_bytes=67043328,
            ),
        )(weight, grad_in, mom_first, mom_second, stat_left, stat_right, basis_left, basis_right)

    return jax.shard_map(local_step, mesh=mesh, in_specs=(tile_spec,) * 8, out_specs=(tile_spec,) * 5, check_vma=False)
```

time: 520 us -> 185 us (0.36)
  the two profiles are of different devices: /device:TPU:0 before, /device:TPU:18 now
where the time goes in v1:
time: 185 us
  Pallas kernels  174 us (94%)
  local copies, waits for them, and re-layouts  9.79 us (5%)
    pallas_call x1, Pallas kernels, local_step(): pl.pallas_call(kernel, name='soap_step', out_shape=[jax.ShapeDtypeStruct(...  174 us
    unnamed x9, local copies, waits for them, and re-layouts  9.79 us

profile of v1, /device:TPU:18, one launch (start us, length us, event | category | flops | bytes accessed | tf_op | source)
XLA Modules:
  0.0 184.9 jit_solution(240018453093153820)
XLA Ops:
  0.6 174.4 %soap_step.1 = (f32[256,1024]{1,0:T(8,128)}, f32[256,1024]{1,0:T(8,128)}, f32[256,1024]{1,0:T(8,128)}, f32[256,256]{1,0:T(8,128)}, f32[1024,1024]{1,0:T(8,128)}) custom-call(f32[256,1024]{1,0:T(8,128)} %w_hbm.1, f32[256,1024]{1,0:T(8,128)} %g_hbm.1, f32[256,1024]{1,0:T(8,128)} %m_hbm.1, f32[256,1024]{1,0:T(8,128)} %v_hbm.1, f32[256,256]{1,0:T(8,128)} %l_hbm.1, ...), custom_call_target="tpu_custom_call" | custom-call | tf_op jit(solution)/shard_map/soap_step/pallas_call | solution.py:477
  175.1 0.0 copy-start.1
  175.1 0.0 copy-start
  175.1 2.5 %copy.18 = f32[256,1024]{1,0:T(8,128)} copy(f32[256,1024]{1,0:T(8,128)} %get-tuple-element.10) | data formatting | bytes 2097152
  177.6 2.3 %copy.19 = f32[256,1024]{1,0:T(8,128)} copy(f32[256,1024]{1,0:T(8,128)} %get-tuple-element.11) | data formatting | bytes 2097152
  179.9 2.3 %copy.20 = f32[256,1024]{1,0:T(8,128)} copy(f32[256,1024]{1,0:T(8,128)} %get-tuple-element.12) | data formatting | bytes 2097152
  182.2 0.0 copy-done.1
  182.2 0.7 copy.21
  182.9 0.0 copy-done
  182.9 2.0 %copy.22 = f32[1024,1024]{1,0:T(8,128)} copy(f32[1024,1024]{1,0:T(8,128)S(1)} %copy-done) | data formatting | bytes 8388608
Async XLA Ops:
  175.1 7.1 %copy-start.1 = (f32[256,256]{1,0:T(8,128)S(1)}, f32[256,256]{1,0:T(8,128)}, u32[]{:S(2)}) copy-start(f32[256,256]{1,0:T(8,128)} %get-tuple-element.13) | copy-start | bytes 786436
  175.1 7.8 %copy-start = (f32[1024,1024]{1,0:T(8,128)S(1)}, f32[1024,1024]{1,0:T(8,128)}, u32[]{:S(2)}) copy-start(f32[1024,1024]{1,0:T(8,128)} %get-tuple-element.14) | copy-start | bytes 12582916

commit v2 on v1

--- a/solution.py
+++ b/solution.py
@@ -19,8 +19,10 @@
 NQ = 4
 NH = 2
 NU = 2
+NG = 2
 NDEV = 4
 NSEND = 160
+VMEM_BYTES = 54 * 2**20
 
 ROWS_T = (((0,), (0,)), ((), ()))
 COLS_T = (((1,), (1,)), ((), ()))
@@ -36,9 +38,9 @@
 
 def kernel(
     w_hbm, g_hbm, m_hbm, v_hbm, l_hbm, r_hbm, ql_hbm, qr_hbm,
-    w_out, m_out, v_out, l_out, r_out,
-    grow, gbf, gi, gj, qrc, hcol, ncol, gis, gicat, gjcat, racc, ubuf, urecv,
-    wbuf, mbuf, vbuf, qlr, qlc, hacc, kb, qlf, lbuf, lx, lrecv,
+    wbuf, mbuf, vbuf, lbuf, racc,
+    grow, gbf, gi, gj, qrc, hcol, ncol, gis, ubuf, urecv,
+    qlr, qlc, hacc, kb, qlf, lx, lrecv,
     ssem, lsem, r_gbf, r_qlr, r_g32, r_qr, r_qlc, r_h, r_n, r_gj, r_gi, r_u, r_l,
 ):
     lay = lax.axis_index("layer")
@@ -52,14 +54,15 @@
     qrows = tc // NQ
     hcols = tc // NH
     urows = tr // NU
-
-    waits = []
+    grows = tr // NG
+
+    waits, qr_waits = [], []
     count = [0]
 
     def dev(row, col):
         return (lay, col, row)
 
-    def send(src, dst, rsem, row, col, cond=None):
+    def send(src, dst, rsem, row, col, cond=None, held=None):
         n = count[0]
         count[0] += 1
 
@@ -79,7 +82,18 @@
             go()
         else:
             pl.when(cond)(go)
-        waits.append((cond, done))
+        if held is None:
+            waits.append((cond, done))
+        else:
+            held.append(done)
+
+    def settle():
+        for cond, done in waits:
+            if cond is None:
+                done()
+            else:
+                pl.when(cond)(done)
+        waits.clear()
 
     def arrived(dst, rsem, row, col):
         pltpu.make_async_remote_copy(
@@ -163,7 +177,7 @@
     def qr_own(q):
         rows = pl.ds(q * qrows, qrows)
         for row in (opp, sib):
-            send(lambda: qrc.at[i, rows], lambda: qrc.at[i, rows], lambda: r_qr.at[i, q], row, z)
+            send(lambda: qrc.at[i, rows], lambda: qrc.at[i, rows], lambda: r_qr.at[i, q], row, z, held=qr_waits)
 
     line_own(gbf, r_gbf)
     for q in range(NQ):
@@ -179,7 +193,7 @@
     def qr_forward(q):
         rows = pl.ds(q * qrows, qrows)
         arrived(qrc.at[opp, rows], r_qr.at[opp, q], opp, z)
-        send(lambda: qrc.at[opp, rows], lambda: qrc.at[opp, rows], lambda: r_qr.at[opp, q], sib, z)
+        send(lambda: qrc.at[opp, rows], lambda: qrc.at[opp, rows], lambda: r_qr.at[opp, q], sib, z, held=qr_waits)
 
     def h_add(k, q, first=False):
         rows = pl.ds(q * qrows, qrows)
@@ -268,22 +282,13 @@
         direction = (new_first / BIAS_ONE) / (jnp.sqrt(new_second / BIAS_TWO) + EPS)
         ncol[i, :, cols] = direction.astype(BF16)
         own_part(ncol, r_n, n)
-    stores = []
-
-    def store(n, src, dst):
-        cp = pltpu.make_async_copy(src, dst, lsem.at[n])
-        cp.start()
-        stores.append(cp)
-
-    store(11, mbuf, m_out)
-    store(12, vbuf, v_out)
-
-    line_forward(grow, r_g32, 2)
     for row, slot in ((opp, 1), (sib, 0)):
         send(lambda: grow.at[z], lambda slot=slot: gj.at[slot], lambda slot=slot: r_gj.at[slot], row, z)
 
     def gi_send(b, valid):
-        send(lambda: grow.at[b], lambda: gi.at[i], lambda: r_gi.at[i], b, z, jnp.logical_and(valid, b != i))
+        for n in range(NG):
+            rows = pl.ds(n * grows, grows)
+            send(lambda: grow.at[b, rows], lambda: gi.at[i, rows], lambda: r_gi.at[i, n], b, z, jnp.logical_and(valid, b != i))
 
     gi_send(z, z >= 0)
     line_last(grow, r_g32, 1)
@@ -302,13 +307,18 @@
         rows = pl.ds(h * urows, urows)
         send(lambda: ubuf.at[a, rows], lambda: urecv.at[slot, rows], lambda: r_u.at[slot, h], i, col, cond)
 
-    for piece in (3, 0, 2, 1):
+    def u_first(a, to_right):
+        for h in range(NU):
+            if to_right:
+                u_send(a, h, a, z + 1, z == 0)
+            else:
+                u_send(a, h, NDEV if a == NDEV - 2 else a, z - 1, z == NDEV - 1)
+
+    for piece, starts in ((3, ((3, True),)), (0, ((0, False),)), (2, ((2, True),)), (1, ((1, False), (1, True), (2, False)))):
         ubuf[piece] = lax.dot_general(kb[...], qrc[piece], COLS_T, preferred_element_type=F32)
-        for h in range(NU):
-            if piece > 0:
-                u_send(piece, h, piece, z + 1, z == 0)
-            if piece < NDEV - 1:
-                u_send(piece, h, NDEV if piece == NDEV - 2 else piece, z - 1, z == NDEV - 1)
+        for a, to_right in starts:
+            u_first(a, to_right)
+    line_forward(grow, r_g32, 2)
 
     def u_at(a, h, station, to_right):
         rows = pl.ds(h * urows, urows)
@@ -336,100 +346,107 @@
                     u_at(a, h, st, True)
                     u_at(NDEV - 1 - a, h, NDEV - 1 - st, False)
 
-    def to_row():
-        gi[i] = grow[i]
-
-    def gj_forward():
-        arrived(gj.at[1], r_gj.at[1], opp, z)
-        send(lambda: gj.at[1], lambda: gj.at[2], lambda: r_gj.at[2], sib, z)
-
-    def split_gi(k):
-        a0, a1, a2 = split3(gi[k])
-        gis[k, 0] = a0
-        gis[k, 1] = a1
-        gis[k, 2] = a2
-
-    mrows = tr
-
-    def right_add(k, gj_ref, first=False):
-        b0, b1, b2 = split3(gj_ref[...])
-        for n, b in enumerate((b0, b1, b2, b0, b1, b0)):
-            gjcat[pl.ds(n * tr, tr)] = b
-        a = [gis[k, n].T for n in range(3)]
-        for n, t in enumerate((0, 0, 0, 1, 1, 2)):
-            gicat[:, pl.ds(n * tr, tr)] = a[t]
-
+    def gj_split(slot, ref):
+        for t, term in enumerate(split3(ref[...])):
+            qrc[slot, pl.ds(t * tr, tr)] = term
+
+    def gi_split(k, ref, n):
+        rows = pl.ds(n * grows, grows)
+        for t, term in enumerate(split3(ref[rows])):
+            gis[k, t, rows] = term
+
+    def right_add(k, slot, n, first=False):
         def body(m, carry):
-            rows = pl.ds(pl.multiple_of(m * mrows, mrows), mrows)
-            part = jnp.dot(gicat[rows], gjcat[...], preferred_element_type=F32)
+            rows = pl.ds(pl.multiple_of(m * tr, tr), tr)
+            part = pl.ds(n * grows, grows)
+            a0, a1, a2 = [gis[k, t, part, rows].T for t in range(3)]
+            b0, b1, b2 = [qrc[slot, pl.ds(t * tr + n * grows, grows)] for t in range(3)]
+            left = jnp.concatenate([a0, a0, a0, a1, a1, a2], axis=1)
+            right = jnp.concatenate([b0, b1, b2, b0, b1, b0], axis=0)
+            share = (1.0 - BETA2) * jnp.dot(left, right, preferred_element_type=F32)
             old = racc[rows]
-            racc[rows] = (BETA2 * old if first else old) + (1.0 - BETA2) * part
+            racc[rows] = (BETA2 * old if first else old) + share
             return carry
 
-        lax.fori_loop(0, tc // mrows, body, 0)
-
-    u_round(1)
-    line_last(grow, r_g32, 3)
-    gi_send(z - 3, z >= 3)
-    gi_send(z + 3, z + 3 < NDEV)
-    to_row()
-    gj_forward()
-    loads["r"].wait()
-    split_gi(i)
-    right_add(i, grow.at[z], first=True)
-
-    def gi_wait(row):
-        arrived(gi.at[row], r_gi.at[row], row, z)
-        split_gi(row)
-
-    gi_wait(sib)
-    arrived(gj.at[0], r_gj.at[0], sib, z)
-    right_add(sib, gj.at[0])
-    u_round(2)
-    gi_wait(opp)
-    right_add(opp, gj.at[1])
-    gi_wait(dia)
-
-    def left_part(k, n):
+        lax.fori_loop(0, tc // tr, body, 0)
+
+    def gi_arrived(row, n):
+        rows = pl.ds(n * grows, grows)
+        arrived(gi.at[row, rows], r_gi.at[row, n], row, z)
+        gi_split(row, gi.at[row], n)
+
+    def left_part(k, slot):
         pieces = [gis[k, t] for t in range(3)]
         other = [gis[z, t] for t in range(3)]
         total = None
         for t, u in ((0, 0), (0, 1), (1, 0), (1, 1), (0, 2), (2, 0)):
             d = lax.dot_general(pieces[t], other[u], COLS_T, preferred_element_type=F32)
             total = d if total is None else total + d
-        lx[n] = total
+        lx[slot] = total
+
+    for done in qr_waits:
+        done()
+    gj_split(0, grow.at[z])
+    arrived(gj.at[0], r_gj.at[0], sib, z)
+    gj_split(1, gj.at[0])
+    arrived(gj.at[1], r_gj.at[1], opp, z)
+    send(lambda: gj.at[1], lambda: gj.at[2], lambda: r_gj.at[2], sib, z)
+    gj_split(2, gj.at[1])
+    u_round(1)
+    line_last(grow, r_g32, 3)
+    gi_send(z - 3, z >= 3)
+    gi_send(z + 3, z + 3 < NDEV)
+    arrived(gj.at[2], r_gj.at[2], sib, z)
+    gj_split(3, gj.at[2])
+    loads["r"].wait()
+    for n in range(NG):
+        gi_split(i, grow.at[i], n)
+        right_add(i, 0, n, first=n == 0)
+    u_round(2)
+    for n in range(NG):
+        gi_arrived(sib, n)
+        right_add(sib, 1, n)
+    for n in range(NG - 1):
+        gi_arrived(opp, n)
+        right_add(opp, 2, n)
+        gi_arrived(dia, n)
+        right_add(dia, 3, n)
+    loads["w"].wait()
+    loads["l"].wait()
+    gi_arrived(dia, NG - 1)
+    gi_arrived(opp, NG - 1)
 
     left_part(dia, 3)
+    send(lambda: lx.at[3], lambda: lrecv.at[2], lambda: r_l.at[2], sib, z)
     left_part(opp, 2)
-    send(lambda: lx.at[3], lambda: lrecv.at[2], lambda: r_l.at[2], dia, z)
+    left_part(sib, 1)
+    send(lambda: lx.at[1], lambda: lrecv.at[0], lambda: r_l.at[0], sib, z)
+    arrived(lrecv.at[2], r_l.at[2], sib, z)
+    lx[2] += lrecv[2]
+    left_part(i, 0)
     send(lambda: lx.at[2], lambda: lrecv.at[1], lambda: r_l.at[1], opp, z)
-    left_part(sib, 1)
-    left_part(i, 0)
-    send(lambda: lx.at[1], lambda: lrecv.at[0], lambda: r_l.at[0], sib, z)
-
-    arrived(gj.at[2], r_gj.at[2], sib, z)
-    right_add(dia, gj.at[2])
-    store(13, racc, r_out)
-    loads["w"].wait()
+    right_add(opp, 2, NG - 1)
+    right_add(dia, 3, NG - 1)
+
     u_round(3)
     wbuf[...] = wbuf[...] - LR * ubuf[z]
-    store(14, wbuf, w_out)
-    loads["l"].wait()
     arrived(lrecv.at[0], r_l.at[0], sib, z)
+    left_sum = lx[0] + lrecv[0]
     arrived(lrecv.at[1], r_l.at[1], opp, z)
-    arrived(lrecv.at[2], r_l.at[2], dia, z)
-    left_sum = (lx[0] + lrecv[0]) + (lrecv[1] + lrecv[2])
+    left_sum += lrecv[1]
     lbuf[...] = BETA2 * lbuf[...] + (1.0 - BETA2) * left_sum
-    store(15, lbuf, l_out)
-
-    for cond, done in waits:
-        if cond is None:
-            done()
-        else:
-            pl.when(cond)(done)
-    for cp in stores:
+
+    settle()
+    assert count[0] <= NSEND, count[0]
+
+
+def write_out(*refs):
+    ins, outs, sem = refs[:5], refs[5:10], refs[10]
+    copies = [pltpu.make_async_copy(a, b, sem.at[n]) for n, (a, b) in enumerate(zip(ins, outs))]
+    for cp in copies:
+        cp.start()
+    for cp in copies:
         cp.wait()
-    assert count[0] <= NSEND, count[0]
 
 
 def solution(mesh):
@@ -448,19 +465,12 @@
             pltpu.VMEM((4, tr, tc), BF16),
             pltpu.VMEM((4, tr, tc), BF16),
             pltpu.VMEM((4, 3, tr, tc), BF16),
-            pltpu.VMEM((tc, 6 * tr), BF16),
-            pltpu.VMEM((6 * tr, tc), BF16),
-            pltpu.VMEM((tc, tc), F32),
             pltpu.VMEM((4, tr, tc), F32),
             pltpu.VMEM((5, tr, tc), F32),
-            pltpu.VMEM((tr, tc), F32),
-            pltpu.VMEM((tr, tc), F32),
-            pltpu.VMEM((tr, tc), F32),
             pltpu.VMEM((4, tl, tl), BF16),
             pltpu.VMEM((4, tl, tl), BF16),
             pltpu.VMEM((tr, tc), F32),
             pltpu.VMEM((tr, tc), BF16),
-            pltpu.VMEM((tl, tl), F32),
             pltpu.VMEM((tl, tl), F32),
             pltpu.VMEM((4, tl, tl), F32),
             pltpu.VMEM((3, tl, tl), F32),
@@ -469,21 +479,32 @@
             dma((4,)), dma((4,)), dma((4,)),
             dma((4, NQ)), dma((4,)),
             dma((4, NH)), dma((4, NH)),
-            dma((3,)), dma((4,)),
+            dma((3,)), dma((4, NG)),
             dma((5, NU)), dma((3,)),
         ]
         any_spec = pl.BlockSpec(memory_space=pl.ANY)
+        vmem_spec = pl.BlockSpec(memory_space=pltpu.VMEM)
         outs = [weight, mom_first, mom_second, stat_left, stat_right]
-        return pl.pallas_call(
+        results = pl.pallas_call(
             kernel,
             name="soap_step",
-            out_shape=[jax.ShapeDtypeStruct(o.shape, o.dtype) for o in outs],
+            out_shape=[pltpu.VMEM(o.shape, o.dtype) for o in outs],
             in_specs=[any_spec] * 8,
-            out_specs=[any_spec] * 5,
+            out_specs=[vmem_spec] * 5,
             scratch_shapes=scratch,
             compiler_params=pltpu.CompilerParams(
-                collective_id=0, has_side_effects=True, vmem_limit_bytes=67043328,
+                collective_id=0, has_side_effects=True, vmem_limit_bytes=VMEM_BYTES,
             ),
         )(weight, grad_in, mom_first, mom_second, stat_left, stat_right, basis_left, basis_right)
+        results = [pltpu.with_memory_space_constraint(r, pltpu.VMEM) for r in results]
+        return pl.pallas_call(
+            write_out,
+            name="write_out",
+            out_shape=[jax.ShapeDtypeStruct(o.shape, o.dtype) for o in outs],
+            in_specs=[vmem_spec] * 5,
+            out_specs=[any_spec] * 5,
+            scratch_shapes=[dma((5,))],
+            compiler_params=pltpu.CompilerParams(vmem_limit_bytes=2**20),
+        )(*results)
 
     return jax.shard_map(local_step, mesh=mesh, in_specs=(tile_spec,) * 8, out_specs=(tile_spec,) * 5, check_vma=False)

time: 185 us -> 165 us (0.89)
  the two profiles are of different devices: /device:TPU:18 before, /device:TPU:0 now
where the time goes in v2:
time: 165 us
  Pallas kernels  164 us (99%)
    pallas_call x1, Pallas kernels, local_step(): pl.pallas_call(kernel, name='soap_step', out_shape=[pltpu.VMEM(o.shape, o...  161 us

profile of v2, /device:TPU:0, one launch (start us, length us, event | category | flops | bytes accessed | tf_op | source)
XLA Modules:
  0.0 164.8 jit_solution(13698730547398103157)
XLA Ops:
  0.6 160.8 %soap_step.1 = (f32[256,1024]{1,0:T(8,128)S(1)}, f32[256,1024]{1,0:T(8,128)S(1)}, f32[256,1024]{1,0:T(8,128)S(1)}, f32[256,256]{1,0:T(8,128)S(1)}, f32[1024,1024]{1,0:T(8,128)S(1)}) custom-call(f32[256,1024]{1,0:T(8,128)} %w_hbm.1, f32[256,1024]{1,0:T(8,128)} %g_hbm.1, f32[256,1024]{1,0:T(8,128)} %m_hbm.1, f32[256,1024]{1,0:T(8,128)} %v_hbm.1, ...), custom_call_target="tpu_custom_call" | custom-call | tf_op jit(solution)/shard_map/soap_step/pallas_call | solution.py:488
  161.4 3.2 %write_out.1 = (f32[256,1024]{1,0:T(8,128)}, f32[256,1024]{1,0:T(8,128)}, f32[256,1024]{1,0:T(8,128)}, f32[256,256]{1,0:T(8,128)}, f32[1024,1024]{1,0:T(8,128)}) custom-call(f32[256,1024]{1,0:T(8,128)S(1)} %get-tuple-element.10.refs_0_, f32[256,1024]{1,0:T(8,128)S(1)} %get-tuple-element.11.refs_1_, f32[256,1024]{1,0:T(8,128)S(1)} %get-tuple-element.12.refs_2_, ...), custom_call_target="tpu_custom_call" | custom-call | tf_op jit(solution)/shard_map/write_out/pallas_call | solution.py:500

commit v3 on v2

--- a/solution.py
+++ b/solution.py
@@ -40,8 +40,8 @@
     w_hbm, g_hbm, m_hbm, v_hbm, l_hbm, r_hbm, ql_hbm, qr_hbm,
     wbuf, mbuf, vbuf, lbuf, racc,
     grow, gbf, gi, gj, qrc, hcol, ncol, gis, ubuf, urecv,
-    qlr, qlc, hacc, kb, qlf, lx, lrecv,
-    ssem, lsem, r_gbf, r_qlr, r_g32, r_qr, r_qlc, r_h, r_n, r_gj, r_gi, r_u, r_l,
+    qlr, qlc, hacc, kb, qrx, kx, qlf, lx, lrecv,
+    ssem, lsem, r_gbf, r_qlr, r_g32, r_qr, r_qlc, r_h, r_n, r_gj, r_gi, r_u, r_qx, r_l,
 ):
     lay = lax.axis_index("layer")
     z = lax.axis_index("col")
@@ -55,8 +55,9 @@
     hcols = tc // NH
     urows = tr // NU
     grows = tr // NG
-
-    waits, qr_waits = [], []
+    early = tc - tc // 4
+
+    waits, qr_waits, late_waits = [], [], []
     count = [0]
 
     def dev(row, col):
@@ -85,15 +86,15 @@
         if held is None:
             waits.append((cond, done))
         else:
-            held.append(done)
-
-    def settle():
-        for cond, done in waits:
+            held.append((cond, done))
+
+    def settle(sent):
+        for cond, done in sent:
             if cond is None:
                 done()
             else:
                 pl.when(cond)(done)
-        waits.clear()
+        sent.clear()
 
     def arrived(dst, rsem, row, col):
         pltpu.make_async_remote_copy(
@@ -108,11 +109,12 @@
         cp.start()
         loads[name] = cp
 
-    load("g", 0, g_hbm, grow.at[z])
     for q in range(NQ):
         rows = pl.ds(q * qrows, qrows)
         load(("qr", q), 1 + q, qr_hbm.at[rows], racc.at[rows])
-    load("ql", 5, ql_hbm, qlf)
+        if q == 0:
+            load("g", 0, g_hbm, grow.at[z])
+            load("ql", 5, ql_hbm, qlf)
     load("m", 6, m_hbm, mbuf)
     load("v", 7, v_hbm, vbuf)
     load("w", 8, w_hbm, wbuf)
@@ -130,6 +132,15 @@
     def _():
         pl.semaphore_signal(barrier, inc=1, device_id=dev(i, z + 1), device_id_type=MESH)
 
+    def qr_cast(q):
+        rows = pl.ds(q * qrows, qrows)
+        loads[("qr", q)].wait()
+        qrc[i, rows] = racc[rows].astype(BF16)
+
+    qr_cast(0)
+    loads["g"].wait()
+    gbf[z] = grow[z].astype(BF16)
+
     inner = jnp.logical_and(z > 0, z < NDEV - 1)
 
     @pl.when(inner)
@@ -169,25 +180,20 @@
         def _():
             arrived(buf.at[z + s], rs.at[z + s], i, z + 1)
 
-    loads["g"].wait()
-    gbf[z] = grow[z].astype(BF16)
+    def qr_own(q):
+        rows = pl.ds(q * qrows, qrows)
+        for row in (opp, sib):
+            send(lambda: qrc.at[i, rows], lambda: qrc.at[i, rows], lambda: r_qr.at[i, q], row, z, held=qr_waits)
+
+    qr_own(0)
+    line_own(gbf, r_gbf)
     loads["ql"].wait()
     qlr[z] = qlf[...].astype(BF16)
-
-    def qr_own(q):
-        rows = pl.ds(q * qrows, qrows)
-        for row in (opp, sib):
-            send(lambda: qrc.at[i, rows], lambda: qrc.at[i, rows], lambda: r_qr.at[i, q], row, z, held=qr_waits)
-
-    line_own(gbf, r_gbf)
-    for q in range(NQ):
-        rows = pl.ds(q * qrows, qrows)
-        loads[("qr", q)].wait()
-        qrc[i, rows] = racc[rows].astype(BF16)
-        if q == 1:
-            line_own(qlr, r_qlr)
-        if q >= 1:
-            qr_own(q - 1)
+    qr_cast(1)
+    line_own(qlr, r_qlr)
+    for q in range(2, NQ):
+        qr_cast(q)
+        qr_own(q - 1)
     load("r", 10, r_hbm, racc)
 
     def qr_forward(q):
@@ -259,6 +265,11 @@
     hcol[i] = hacc[...].astype(BF16)
     for n in range(NH):
         own_part(hcol, r_h, n)
+
+    half = pl.ds(pl.multiple_of(c * (tc // 2), tc // 2), tc // 2)
+    other_half = pl.ds(pl.multiple_of((1 - c) * (tc // 2), tc // 2), tc // 2)
+    send(lambda: qrc.at[1, half], lambda: qrx.at[half], lambda: r_qx.at[0], i, 1, z == 0, held=qr_waits)
+    send(lambda: qrc.at[2, half], lambda: qrx.at[half], lambda: r_qx.at[0], i, 2, z == 3, held=qr_waits)
 
     line_forward(grow, r_g32, 1)
     for row in (opp, dia, sib):
@@ -282,8 +293,13 @@
         direction = (new_first / BIAS_ONE) / (jnp.sqrt(new_second / BIAS_TWO) + EPS)
         ncol[i, :, cols] = direction.astype(BF16)
         own_part(ncol, r_n, n)
-    for row, slot in ((opp, 1), (sib, 0)):
-        send(lambda: grow.at[z], lambda slot=slot: gj.at[slot], lambda slot=slot: r_gj.at[slot], row, z)
+    def gj_part(src, slot, late):
+        cols = pl.ds(early, tc - early) if late else pl.ds(0, early)
+        n = slot + 2 * late
+        return (lambda: src.at[:, cols]), (lambda: gj.at[slot, :, cols]), (lambda: r_gj.at[n])
+
+    send(*gj_part(grow.at[z], 1, False), opp, z)
+    send(lambda: grow.at[z], lambda: gj.at[0], lambda: r_gj.at[0], sib, z)
 
     def gi_send(b, valid):
         for n in range(NG):
@@ -314,11 +330,19 @@
             else:
                 u_send(a, h, NDEV if a == NDEV - 2 else a, z - 1, z == NDEV - 1)
 
-    for piece, starts in ((3, ((3, True),)), (0, ((0, False),)), (2, ((2, True),)), (1, ((1, False), (1, True), (2, False)))):
+    for piece, starts in ((3, ((3, True),)), (0, ((0, False),)), (2, ((2, True),)), (1, ((1, False),))):
         ubuf[piece] = lax.dot_general(kb[...], qrc[piece], COLS_T, preferred_element_type=F32)
         for a, to_right in starts:
             u_first(a, to_right)
+    send(lambda: kb, lambda: kx, lambda: r_qx.at[2], i, 1, z == 0)
+    send(lambda: kb, lambda: kx, lambda: r_qx.at[2], i, 2, z == 3)
     line_forward(grow, r_g32, 2)
+
+    @pl.when(inner)
+    def _():
+        arrived(qrx.at[half], r_qx.at[0], i, 3 * (z // 2))
+
+    send(lambda: qrx.at[half], lambda: qrx.at[half], lambda: r_qx.at[1], sib, z, inner)
 
     def u_at(a, h, station, to_right):
         rows = pl.ds(h * urows, urows)
@@ -342,30 +366,33 @@
         for h in range(NU):
             for a in (3, 2, 1):
                 st = t - (3 - a)
-                if 1 <= st <= a:
+                if 1 <= st <= a and a > 1:
                     u_at(a, h, st, True)
                     u_at(NDEV - 1 - a, h, NDEV - 1 - st, False)
 
-    def gj_split(slot, ref):
-        for t, term in enumerate(split3(ref[...])):
-            qrc[slot, pl.ds(t * tr, tr)] = term
+    def gj_split(slot, ref, start=0, size=None):
+        cols = pl.ds(start, size or tc)
+        for t, term in enumerate(split3(ref[:, cols])):
+            qrc[slot, pl.ds(t * tr, tr), cols] = term
 
     def gi_split(k, ref, n):
         rows = pl.ds(n * grows, grows)
         for t, term in enumerate(split3(ref[rows])):
             gis[k, t, rows] = term
 
-    def right_add(k, slot, n, first=False):
+    def right_add(k, slot, n=None, start=0, size=None, first=False):
+        begin, depth = (0, tr) if n is None else (n * grows, grows)
+        cols = pl.ds(start, size or tc)
+
         def body(m, carry):
             rows = pl.ds(pl.multiple_of(m * tr, tr), tr)
-            part = pl.ds(n * grows, grows)
-            a0, a1, a2 = [gis[k, t, part, rows].T for t in range(3)]
-            b0, b1, b2 = [qrc[slot, pl.ds(t * tr + n * grows, grows)] for t in range(3)]
+            a0, a1, a2 = [gis[k, t, pl.ds(begin, depth), rows].T for t in range(3)]
+            b0, b1, b2 = [qrc[slot, pl.ds(t * tr + begin, depth), cols] for t in range(3)]
             left = jnp.concatenate([a0, a0, a0, a1, a1, a2], axis=1)
             right = jnp.concatenate([b0, b1, b2, b0, b1, b0], axis=0)
             share = (1.0 - BETA2) * jnp.dot(left, right, preferred_element_type=F32)
-            old = racc[rows]
-            racc[rows] = (BETA2 * old if first else old) + share
+            old = racc[rows, cols]
+            racc[rows, cols] = (BETA2 * old if first else old) + share
             return carry
 
         lax.fori_loop(0, tc // tr, body, 0)
@@ -384,33 +411,40 @@
             total = d if total is None else total + d
         lx[slot] = total
 
-    for done in qr_waits:
-        done()
+    settle(qr_waits)
     gj_split(0, grow.at[z])
     arrived(gj.at[0], r_gj.at[0], sib, z)
     gj_split(1, gj.at[0])
-    arrived(gj.at[1], r_gj.at[1], opp, z)
-    send(lambda: gj.at[1], lambda: gj.at[2], lambda: r_gj.at[2], sib, z)
-    gj_split(2, gj.at[1])
+    arrived(gj.at[1, :, pl.ds(0, early)], r_gj.at[1], opp, z)
+    send(*gj_part(gj.at[1], 2, False), sib, z)
+    gj_split(2, gj.at[1], 0, early)
     u_round(1)
     line_last(grow, r_g32, 3)
     gi_send(z - 3, z >= 3)
     gi_send(z + 3, z + 3 < NDEV)
-    arrived(gj.at[2], r_gj.at[2], sib, z)
-    gj_split(3, gj.at[2])
+    send(*gj_part(grow.at[z], 1, True), opp, z, held=late_waits)
+    arrived(gj.at[2, :, pl.ds(0, early)], r_gj.at[2], sib, z)
+    gj_split(3, gj.at[2], 0, early)
     loads["r"].wait()
     for n in range(NG):
         gi_split(i, grow.at[i], n)
-        right_add(i, 0, n, first=n == 0)
+    right_add(i, 0, first=True)
     u_round(2)
     for n in range(NG):
         gi_arrived(sib, n)
-        right_add(sib, 1, n)
+    right_add(sib, 1)
     for n in range(NG - 1):
         gi_arrived(opp, n)
-        right_add(opp, 2, n)
+        right_add(opp, 2, n, 0, early)
         gi_arrived(dia, n)
-        right_add(dia, 3, n)
+        right_add(dia, 3, n, 0, early)
+
+    @pl.when(inner)
+    def _():
+        arrived(qrx.at[other_half], r_qx.at[1], sib, z)
+        arrived(kx, r_qx.at[2], i, 3 * (z // 2))
+        ubuf[z] += lax.dot_general(kx[...], qrx[...], COLS_T, preferred_element_type=F32)
+
     loads["w"].wait()
     loads["l"].wait()
     gi_arrived(dia, NG - 1)
@@ -424,19 +458,28 @@
     arrived(lrecv.at[2], r_l.at[2], sib, z)
     lx[2] += lrecv[2]
     left_part(i, 0)
-    send(lambda: lx.at[2], lambda: lrecv.at[1], lambda: r_l.at[1], opp, z)
-    right_add(opp, 2, NG - 1)
-    right_add(dia, 3, NG - 1)
+    send(lambda: lx.at[2], lambda: lrecv.at[1], lambda: r_l.at[1], opp, z, held=late_waits)
+    right_add(opp, 2, NG - 1, 0, early)
+    arrived(gj.at[1, :, pl.ds(early, tc - early)], r_gj.at[3], opp, z)
+    send(*gj_part(gj.at[1], 2, True), sib, z, held=late_waits)
+    right_add(dia, 3, NG - 1, 0, early)
+    gj_split(2, gj.at[1], early, tc - early)
+    right_add(opp, 2, None, early, tc - early)
 
     u_round(3)
     wbuf[...] = wbuf[...] - LR * ubuf[z]
+    settle(waits)
+    arrived(gj.at[2, :, pl.ds(early, tc - early)], r_gj.at[4], sib, z)
+    gj_split(3, gj.at[2], early, tc - early)
+    right_add(dia, 3, None, early, tc - early)
     arrived(lrecv.at[0], r_l.at[0], sib, z)
     left_sum = lx[0] + lrecv[0]
     arrived(lrecv.at[1], r_l.at[1], opp, z)
     left_sum += lrecv[1]
     lbuf[...] = BETA2 * lbuf[...] + (1.0 - BETA2) * left_sum
 
-    settle()
+    settle(waits)
+    settle(late_waits)
     assert count[0] <= NSEND, count[0]
 
 
@@ -471,6 +514,8 @@
             pltpu.VMEM((4, tl, tl), BF16),
             pltpu.VMEM((tr, tc), F32),
             pltpu.VMEM((tr, tc), BF16),
+            pltpu.VMEM((tc, tc), BF16),
+            pltpu.VMEM((tr, tc), BF16),
             pltpu.VMEM((tl, tl), F32),
             pltpu.VMEM((4, tl, tl), F32),
             pltpu.VMEM((3, tl, tl), F32),
@@ -479,8 +524,8 @@
             dma((4,)), dma((4,)), dma((4,)),
             dma((4, NQ)), dma((4,)),
             dma((4, NH)), dma((4, NH)),
-            dma((3,)), dma((4, NG)),
-            dma((5, NU)), dma((3,)),
+            dma((5,)), dma((4, NG)),
+            dma((5, NU)), dma((3,)), dma((3,)),
         ]
         any_spec = pl.BlockSpec(memory_space=pl.ANY)
         vmem_spec = pl.BlockSpec(memory_space=pltpu.VMEM)

time: 165 us -> 161 us (0.976)
  Pallas kernels: 164 us -> 160 us
    pallas_call x1, Pallas kernels: 161 us -> 157 us  [local_step(): pl.pallas_call(kernel, name='soap_step', out_shape=[pltpu.VMEM(o.shape, o...]
where the time goes in v3:
time: 161 us
  Pallas kernels  160 us (99%)
    pallas_call x1, Pallas kernels, local_step(): pl.pallas_call(kernel, name='soap_step', out_shape=[pltpu.VMEM(o.shape, o...  157 us

profile of v3, /device:TPU:0, one launch (start us, length us, event | category | flops | bytes accessed | tf_op | source)
XLA Modules:
  0.0 160.6 jit_solution(17958896922283375685)
XLA Ops:
  0.6 156.6 %soap_step.1 = (f32[256,1024]{1,0:T(8,128)S(1)}, f32[256,1024]{1,0:T(8,128)S(1)}, f32[256,1024]{1,0:T(8,128)S(1)}, f32[256,256]{1,0:T(8,128)S(1)}, f32[1024,1024]{1,0:T(8,128)S(1)}) custom-call(f32[256,1024]{1,0:T(8,128)} %w_hbm.1, f32[256,1024]{1,0:T(8,128)} %g_hbm.1, f32[256,1024]{1,0:T(8,128)} %m_hbm.1, f32[256,1024]{1,0:T(8,128)} %v_hbm.1, ...), custom_call_target="tpu_custom_call" | custom-call | tf_op jit(solution)/shard_map/soap_step/pallas_call | solution.py:533
  157.2 3.2 %write_out.1 = (f32[256,1024]{1,0:T(8,128)}, f32[256,1024]{1,0:T(8,128)}, f32[256,1024]{1,0:T(8,128)}, f32[256,256]{1,0:T(8,128)}, f32[1024,1024]{1,0:T(8,128)}) custom-call(f32[256,1024]{1,0:T(8,128)S(1)} %get-tuple-element.10.refs_0_, f32[256,1024]{1,0:T(8,128)S(1)} %get-tuple-element.11.refs_1_, f32[256,1024]{1,0:T(8,128)S(1)} %get-tuple-element.12.refs_2_, ...), custom_call_target="tpu_custom_call" | custom-call | tf_op jit(solution)/shard_map/write_out/pallas_call | solution.py:545

commit v4 on v3

--- a/solution.py
+++ b/solution.py
@@ -21,7 +21,7 @@
 NU = 2
 NG = 2
 NDEV = 4
-NSEND = 160
+NSEND = 69
 VMEM_BYTES = 54 * 2**20
 
 ROWS_T = (((0,), (0,)), ((), ()))
@@ -40,7 +40,7 @@
     w_hbm, g_hbm, m_hbm, v_hbm, l_hbm, r_hbm, ql_hbm, qr_hbm,
     wbuf, mbuf, vbuf, lbuf, racc,
     grow, gbf, gi, gj, qrc, hcol, ncol, gis, ubuf, urecv,
-    qlr, qlc, hacc, kb, qrx, kx, qlf, lx, lrecv,
+    qlr, qlc, hacc, kb, qrx, kx, qlf, lx, lrecv, git,
     ssem, lsem, r_gbf, r_qlr, r_g32, r_qr, r_qlc, r_h, r_n, r_gj, r_gi, r_u, r_qx, r_l,
 ):
     lay = lax.axis_index("layer")
@@ -55,21 +55,23 @@
     hcols = tc // NH
     urows = tr // NU
     grows = tr // NG
+    gparts = (pl.ds(0, grows // 2), pl.ds(grows // 2, grows // 2), pl.ds(grows, grows))
     early = tc - tc // 4
 
-    waits, qr_waits, late_waits = [], [], []
-    count = [0]
+    waits, qr_waits, late_waits, line_waits = [], [], [], []
+    unused, most = list(range(NSEND)), [0]
 
     def dev(row, col):
         return (lay, col, row)
 
     def send(src, dst, rsem, row, col, cond=None, held=None):
-        n = count[0]
-        count[0] += 1
+        src, dst, rsem = src(), dst(), rsem()
+        n = unused.pop(0)
+        most[0] = max(most[0], n + 1)
 
         def make():
             return pltpu.make_async_remote_copy(
-                src_ref=src(), dst_ref=dst(), send_sem=ssem.at[n], recv_sem=rsem(),
+                src_ref=src, dst_ref=dst, send_sem=ssem.at[n], recv_sem=rsem,
                 device_id=dev(row, col), device_id_type=MESH,
             )
 
@@ -84,16 +86,18 @@
         else:
             pl.when(cond)(go)
         if held is None:
-            waits.append((cond, done))
+            waits.append((cond, done, n))
         else:
-            held.append((cond, done))
+            held.append((cond, done, n))
 
     def settle(sent):
-        for cond, done in sent:
+        for cond, done, n in sent:
             if cond is None:
                 done()
             else:
                 pl.when(cond)(done)
+            unused.append(n)
+        unused.sort()
         sent.clear()
 
     def arrived(dst, rsem, row, col):
@@ -138,9 +142,6 @@
         qrc[i, rows] = racc[rows].astype(BF16)
 
     qr_cast(0)
-    loads["g"].wait()
-    gbf[z] = grow[z].astype(BF16)
-
     inner = jnp.logical_and(z > 0, z < NDEV - 1)
 
     @pl.when(inner)
@@ -151,11 +152,11 @@
     def _():
         pl.semaphore_wait(barrier, 4)
 
-    def line_own(buf, rs):
-        send(lambda: buf.at[z], lambda: buf.at[z], lambda: rs.at[z], i, z + 1, z < NDEV - 1)
-        send(lambda: buf.at[z], lambda: buf.at[z], lambda: rs.at[z], i, z - 1, z > 0)
-
-    def line_forward(buf, rs, s):
+    def line_own(buf, rs, held=None):
+        send(lambda: buf.at[z], lambda: buf.at[z], lambda: rs.at[z], i, z + 1, z < NDEV - 1, held)
+        send(lambda: buf.at[z], lambda: buf.at[z], lambda: rs.at[z], i, z - 1, z > 0, held)
+
+    def line_forward(buf, rs, s, held=None):
         right = jnp.logical_and(z >= s, z < NDEV - 1)
         left = jnp.logical_and(z + s < NDEV, z > 0)
 
@@ -163,13 +164,13 @@
         def _():
             arrived(buf.at[z - s], rs.at[z - s], i, z - 1)
 
-        send(lambda: buf.at[z - s], lambda: buf.at[z - s], lambda: rs.at[z - s], i, z + 1, right)
+        send(lambda: buf.at[z - s], lambda: buf.at[z - s], lambda: rs.at[z - s], i, z + 1, right, held)
 
         @pl.when(left)
         def _():
             arrived(buf.at[z + s], rs.at[z + s], i, z + 1)
 
-        send(lambda: buf.at[z + s], lambda: buf.at[z + s], lambda: rs.at[z + s], i, z - 1, left)
+        send(lambda: buf.at[z + s], lambda: buf.at[z + s], lambda: rs.at[z + s], i, z - 1, left, held)
 
     def line_last(buf, rs, s):
         @pl.when(jnp.logical_and(z >= s, z == NDEV - 1))
@@ -186,6 +187,8 @@
             send(lambda: qrc.at[i, rows], lambda: qrc.at[i, rows], lambda: r_qr.at[i, q], row, z, held=qr_waits)
 
     qr_own(0)
+    loads["g"].wait()
+    gbf[z] = grow[z].astype(BF16)
     line_own(gbf, r_gbf)
     loads["ql"].wait()
     qlr[z] = qlf[...].astype(BF16)
@@ -216,7 +219,7 @@
     qr_forward(0)
     line_forward(gbf, r_gbf, 2)
     line_forward(qlr, r_qlr, 2)
-    line_own(grow, r_g32)
+    line_own(grow, r_g32, line_waits)
     qr_forward(1)
     for s in range(1, NDEV):
         line_last(gbf, r_gbf, s)
@@ -271,7 +274,10 @@
     send(lambda: qrc.at[1, half], lambda: qrx.at[half], lambda: r_qx.at[0], i, 1, z == 0, held=qr_waits)
     send(lambda: qrc.at[2, half], lambda: qrx.at[half], lambda: r_qx.at[0], i, 2, z == 3, held=qr_waits)
 
-    line_forward(grow, r_g32, 1)
+    early_waits = waits[:]
+    waits.clear()
+
+    line_forward(grow, r_g32, 1, line_waits)
     for row in (opp, dia, sib):
         arrived(qlc.at[row], r_qlc.at[row], row, z)
     loads["m"].wait()
@@ -298,13 +304,26 @@
         n = slot + 2 * late
         return (lambda: src.at[:, cols]), (lambda: gj.at[slot, :, cols]), (lambda: r_gj.at[n])
 
+    head = gparts[0]
+    ahead = 1 - 2 * y
+
+    def relay(station, came_row, came_col):
+        @pl.when(z == station)
+        def _():
+            arrived(gi.at[opp, head], r_gi.at[opp, 0], came_row, came_col)
+
+        send(lambda: gi.at[opp, head], lambda: gi.at[opp, head], lambda: r_gi.at[opp, 0], i, z + ahead, z == station)
+
+    send(lambda: grow.at[opp, head], lambda: gi.at[i, head], lambda: r_gi.at[i, 0], opp, z, z == 2 - y)
+
     send(*gj_part(grow.at[z], 1, False), opp, z)
     send(lambda: grow.at[z], lambda: gj.at[0], lambda: r_gj.at[0], sib, z)
 
     def gi_send(b, valid):
-        for n in range(NG):
-            rows = pl.ds(n * grows, grows)
-            send(lambda: grow.at[b, rows], lambda: gi.at[i, rows], lambda: r_gi.at[i, n], b, z, jnp.logical_and(valid, b != i))
+        there = jnp.logical_and(valid, b != i)
+        for n, rows in enumerate(gparts):
+            cond = jnp.logical_and(there, jnp.logical_or(b != opp, z == 3 - 3 * y)) if n == 0 else there
+            send(lambda: grow.at[b, rows], lambda: gi.at[i, rows], lambda: r_gi.at[i, n], b, z, cond)
 
     gi_send(z, z >= 0)
     line_last(grow, r_g32, 1)
@@ -319,6 +338,8 @@
             jnp.dot(qlr[k], ncol[k, :, cols], preferred_element_type=F32) for k in range(NDEV)
         ).astype(BF16)
 
+    settle(early_waits)
+
     def u_send(a, h, slot, col, cond):
         rows = pl.ds(h * urows, urows)
         send(lambda: ubuf.at[a, rows], lambda: urecv.at[slot, rows], lambda: r_u.at[slot, h], i, col, cond)
@@ -336,7 +357,9 @@
             u_first(a, to_right)
     send(lambda: kb, lambda: kx, lambda: r_qx.at[2], i, 1, z == 0)
     send(lambda: kb, lambda: kx, lambda: r_qx.at[2], i, 2, z == 3)
-    line_forward(grow, r_g32, 2)
+    line_forward(grow, r_g32, 2, line_waits)
+
+    relay(1 + y, opp, z)
 
     @pl.when(inner)
     def _():
@@ -380,13 +403,16 @@
         for t, term in enumerate(split3(ref[rows])):
             gis[k, t, rows] = term
 
-    def right_add(k, slot, n=None, start=0, size=None, first=False):
+    def right_add(k, slot, n=None, start=0, size=None, first=False, turned=None):
         begin, depth = (0, tr) if n is None else (n * grows, grows)
         cols = pl.ds(start, size or tc)
 
         def body(m, carry):
             rows = pl.ds(pl.multiple_of(m * tr, tr), tr)
-            a0, a1, a2 = [gis[k, t, pl.ds(begin, depth), rows].T for t in range(3)]
+            if turned is None:
+                a0, a1, a2 = [gis[k, t, pl.ds(begin, depth), rows].T for t in range(3)]
+            else:
+                a0, a1, a2 = [git[turned, rows, pl.ds(t * tr + begin, depth)] for t in range(3)]
             b0, b1, b2 = [qrc[slot, pl.ds(t * tr + begin, depth), cols] for t in range(3)]
             left = jnp.concatenate([a0, a0, a0, a1, a1, a2], axis=1)
             right = jnp.concatenate([b0, b1, b2, b0, b1, b0], axis=0)
@@ -397,10 +423,25 @@
 
         lax.fori_loop(0, tc // tr, body, 0)
 
-    def gi_arrived(row, n):
-        rows = pl.ds(n * grows, grows)
-        arrived(gi.at[row, rows], r_gi.at[row, n], row, z)
+    def gi_arrived(row, n, turned=None):
+        if n == 1:
+            arrived(gi.at[row, gparts[2]], r_gi.at[row, 2], row, z)
+        else:
+            arrived(gi.at[row, gparts[1]], r_gi.at[row, 1], row, z)
+            if row is opp:
+                @pl.when(z == 3 * y)
+                def _():
+                    arrived(gi.at[row, head], r_gi.at[row, 0], row, z)
+
+                @pl.when(z == 3 - 3 * y)
+                def _():
+                    arrived(gi.at[row, head], r_gi.at[row, 0], i, z - ahead)
+            else:
+                arrived(gi.at[row, head], r_gi.at[row, 0], row, z)
         gi_split(row, gi.at[row], n)
+        if turned is not None:
+            for t in range(3):
+                git[turned, :, pl.ds(t * tr + n * grows, grows)] = gis[row, t, pl.ds(n * grows, grows)].T
 
     def left_part(k, slot):
         pieces = [gis[k, t] for t in range(3)]
@@ -417,6 +458,7 @@
     gj_split(1, gj.at[0])
     arrived(gj.at[1, :, pl.ds(0, early)], r_gj.at[1], opp, z)
     send(*gj_part(gj.at[1], 2, False), sib, z)
+    relay(2 - y, i, z - ahead)
     gj_split(2, gj.at[1], 0, early)
     u_round(1)
     line_last(grow, r_g32, 3)
@@ -434,10 +476,10 @@
         gi_arrived(sib, n)
     right_add(sib, 1)
     for n in range(NG - 1):
-        gi_arrived(opp, n)
-        right_add(opp, 2, n, 0, early)
-        gi_arrived(dia, n)
-        right_add(dia, 3, n, 0, early)
+        gi_arrived(opp, n, 0)
+        right_add(opp, 2, n, 0, early, turned=0)
+        gi_arrived(dia, n, 1)
+        right_add(dia, 3, n, 0, early, turned=1)
 
     @pl.when(inner)
     def _():
@@ -447,8 +489,8 @@
 
     loads["w"].wait()
     loads["l"].wait()
-    gi_arrived(dia, NG - 1)
-    gi_arrived(opp, NG - 1)
+    gi_arrived(dia, NG - 1, 1)
+    gi_arrived(opp, NG - 1, 0)
 
     left_part(dia, 3)
     send(lambda: lx.at[3], lambda: lrecv.at[2], lambda: r_l.at[2], sib, z)
@@ -457,21 +499,22 @@
     send(lambda: lx.at[1], lambda: lrecv.at[0], lambda: r_l.at[0], sib, z)
     arrived(lrecv.at[2], r_l.at[2], sib, z)
     lx[2] += lrecv[2]
+    send(lambda: lx.at[2], lambda: lrecv.at[1], lambda: r_l.at[1], opp, z, held=late_waits)
     left_part(i, 0)
-    send(lambda: lx.at[2], lambda: lrecv.at[1], lambda: r_l.at[1], opp, z, held=late_waits)
-    right_add(opp, 2, NG - 1, 0, early)
+    right_add(opp, 2, NG - 1, 0, early, turned=0)
     arrived(gj.at[1, :, pl.ds(early, tc - early)], r_gj.at[3], opp, z)
     send(*gj_part(gj.at[1], 2, True), sib, z, held=late_waits)
-    right_add(dia, 3, NG - 1, 0, early)
+    right_add(dia, 3, NG - 1, 0, early, turned=1)
     gj_split(2, gj.at[1], early, tc - early)
-    right_add(opp, 2, None, early, tc - early)
+    right_add(opp, 2, None, early, tc - early, turned=0)
 
     u_round(3)
     wbuf[...] = wbuf[...] - LR * ubuf[z]
     settle(waits)
+    settle(line_waits)
     arrived(gj.at[2, :, pl.ds(early, tc - early)], r_gj.at[4], sib, z)
     gj_split(3, gj.at[2], early, tc - early)
-    right_add(dia, 3, None, early, tc - early)
+    right_add(dia, 3, None, early, tc - early, turned=1)
     arrived(lrecv.at[0], r_l.at[0], sib, z)
     left_sum = lx[0] + lrecv[0]
     arrived(lrecv.at[1], r_l.at[1], opp, z)
@@ -480,12 +523,17 @@
 
     settle(waits)
     settle(late_waits)
-    assert count[0] <= NSEND, count[0]
+    assert most[0] == NSEND, most[0]
 
 
 def write_out(*refs):
     ins, outs, sem = refs[:5], refs[5:10], refs[10]
-    copies = [pltpu.make_async_copy(a, b, sem.at[n]) for n, (a, b) in enumerate(zip(ins, outs))]
+    copies = []
+    for a, b in zip(ins, outs):
+        step = a.shape[0] // 4
+        for n in range(4):
+            rows = pl.ds(n * step, step)
+            copies.append(pltpu.make_async_copy(a.at[rows], b.at[rows], sem.at[len(copies)]))
     for cp in copies:
         cp.start()
     for cp in copies:
@@ -519,12 +567,13 @@
             pltpu.VMEM((tl, tl), F32),
             pltpu.VMEM((4, tl, tl), F32),
             pltpu.VMEM((3, tl, tl), F32),
+            pltpu.VMEM((2, tc, 3 * tr), BF16),
             dma((NSEND,)),
-            dma((16,)),
+            dma((11,)),
             dma((4,)), dma((4,)), dma((4,)),
             dma((4, NQ)), dma((4,)),
             dma((4, NH)), dma((4, NH)),
-            dma((5,)), dma((4, NG)),
+            dma((5,)), dma((4, 3)),
             dma((5, NU)), dma((3,)), dma((3,)),
         ]
         any_spec = pl.BlockSpec(memory_space=pl.ANY)
@@ -548,7 +597,7 @@
             out_shape=[jax.ShapeDtypeStruct(o.shape, o.dtype) for o in outs],
             in_specs=[vmem_spec] * 5,
             out_specs=[any_spec] * 5,
-            scratch_shapes=[dma((5,))],
+            scratch_shapes=[dma((20,))],
             compiler_params=pltpu.CompilerParams(vmem_limit_bytes=2**20),
         )(*results)
 

time: 161 us -> 159 us (0.988)
  Pallas kernels: 160 us -> 157 us
    pallas_call x1, Pallas kernels: 157 us -> 154 us  [local_step(): pl.pallas_call(kernel, name='soap_step', out_shape=[pltpu.VMEM(o.shape, o...]
where the time goes in v4:
time: 159 us; the launch traced here: 158 us
  Pallas kernels  157 us (99%)
    pallas_call x1, Pallas kernels, local_step(): pl.pallas_call(kernel, name='soap_step', out_shape=[pltpu.VMEM(o.shape, o...  154 us
    pallas_call x1, Pallas kernels, local_step(): pl.pallas_call(write_out, name='write_out', out_shape=[jax.ShapeDtypeStru...  3.24 us

profile of v4, /device:TPU:0, one launch (start us, length us, event | category | flops | bytes accessed | tf_op | source)
XLA Modules:
  0.0 158.0 jit_solution(16804710717917575650)
XLA Ops:
  0.6 153.9 %soap_step.1 = (f32[256,1024]{1,0:T(8,128)S(1)}, f32[256,1024]{1,0:T(8,128)S(1)}, f32[256,1024]{1,0:T(8,128)S(1)}, f32[256,256]{1,0:T(8,128)S(1)}, f32[1024,1024]{1,0:T(8,128)S(1)}) custom-call(f32[256,1024]{1,0:T(8,128)} %w_hbm.1, f32[256,1024]{1,0:T(8,128)} %g_hbm.1, f32[256,1024]{1,0:T(8,128)} %m_hbm.1, f32[256,1024]{1,0:T(8,128)} %v_hbm.1, ...), custom_call_target="tpu_custom_call" | custom-call | tf_op jit(solution)/shard_map/soap_step/pallas_call | solution.py:582
  154.6 3.2 %write_out.1 = (f32[256,1024]{1,0:T(8,128)}, f32[256,1024]{1,0:T(8,128)}, f32[256,1024]{1,0:T(8,128)}, f32[256,256]{1,0:T(8,128)}, f32[1024,1024]{1,0:T(8,128)}) custom-call(f32[256,1024]{1,0:T(8,128)S(1)} %get-tuple-element.10.refs_0_, f32[256,1024]{1,0:T(8,128)S(1)} %get-tuple-element.11.refs_1_, f32[256,1024]{1,0:T(8,128)S(1)} %get-tuple-element.12.refs_2_, ...), custom_call_target="tpu_custom_call" | custom-call | tf_op jit(solution)/shard_map/write_out/pallas_call | solution.py:594

commit v5 on v4

--- a/solution.py
+++ b/solution.py
@@ -22,7 +22,7 @@
 NG = 2
 NDEV = 4
 NSEND = 69
-VMEM_BYTES = 54 * 2**20
+VMEM_BYTES = 56 * 2**20
 
 ROWS_T = (((0,), (0,)), ((), ()))
 COLS_T = (((1,), (1,)), ((), ()))
@@ -55,7 +55,8 @@
     hcols = tc // NH
     urows = tr // NU
     grows = tr // NG
-    gparts = (pl.ds(0, grows // 2), pl.ds(grows // 2, grows // 2), pl.ds(grows, grows))
+    head_rows = 3 * grows // 4
+    gparts = (pl.ds(0, head_rows), pl.ds(head_rows, grows - head_rows), pl.ds(grows, grows))
     early = tc - tc // 4
 
     waits, qr_waits, late_waits, line_waits = [], [], [], []
@@ -384,6 +385,7 @@
     line_last(grow, r_g32, 2)
     gi_send(z - 2, z >= 2)
     gi_send(z + 2, z + 2 < NDEV)
+    far = jnp.logical_or(jnp.logical_and(z == 0, i == 3), jnp.logical_and(z == 3, i == 0))
 
     def u_round(t):
         for h in range(NU):
@@ -456,6 +458,17 @@
     gj_split(0, grow.at[z])
     arrived(gj.at[0], r_gj.at[0], sib, z)
     gj_split(1, gj.at[0])
+    loads["r"].wait()
+
+    def chip_rows():
+        for n in range(NG):
+            gi_split(i, grow.at[i], n)
+        right_add(i, 0, first=True)
+        for n in range(NG):
+            gi_arrived(sib, n)
+        right_add(sib, 1)
+
+    pl.when(jnp.logical_not(far))(chip_rows)
     arrived(gj.at[1, :, pl.ds(0, early)], r_gj.at[1], opp, z)
     send(*gj_part(gj.at[1], 2, False), sib, z)
     relay(2 - y, i, z - ahead)
@@ -467,14 +480,8 @@
     send(*gj_part(grow.at[z], 1, True), opp, z, held=late_waits)
     arrived(gj.at[2, :, pl.ds(0, early)], r_gj.at[2], sib, z)
     gj_split(3, gj.at[2], 0, early)
-    loads["r"].wait()
-    for n in range(NG):
-        gi_split(i, grow.at[i], n)
-    right_add(i, 0, first=True)
+    pl.when(far)(chip_rows)
     u_round(2)
-    for n in range(NG):
-        gi_arrived(sib, n)
-    right_add(sib, 1)
     for n in range(NG - 1):
         gi_arrived(opp, n, 0)
         right_add(opp, 2, n, 0, early, turned=0)

time: 159 us -> 159 us (level)
  no operation moved by 1% of the time
where the time goes in v5:
time: 159 us; the launch traced here: 158 us
  Pallas kernels  157 us (99%)
    pallas_call x1, Pallas kernels, local_step(): pl.pallas_call(kernel, name='soap_step', out_shape=[pltpu.VMEM(o.shape, o...  154 us
    pallas_call x1, Pallas kernels, local_step(): pl.pallas_call(write_out, name='write_out', out_shape=[jax.ShapeDtypeStru...  3.24 us

profile of v5, /device:TPU:0, one launch (start us, length us, event | category | flops | bytes accessed | tf_op | source)
XLA Modules:
  0.0 158.0 jit_solution(10918109512933379477)
XLA Ops:
  0.6 153.9 %soap_step.1 = (f32[256,1024]{1,0:T(8,128)S(1)}, f32[256,1024]{1,0:T(8,128)S(1)}, f32[256,1024]{1,0:T(8,128)S(1)}, f32[256,256]{1,0:T(8,128)S(1)}, f32[1024,1024]{1,0:T(8,128)S(1)}) custom-call(f32[256,1024]{1,0:T(8,128)} %w_hbm.1, f32[256,1024]{1,0:T(8,128)} %g_hbm.1, f32[256,1024]{1,0:T(8,128)} %m_hbm.1, f32[256,1024]{1,0:T(8,128)} %v_hbm.1, ...), custom_call_target="tpu_custom_call" | custom-call | tf_op jit(solution)/shard_map/soap_step/pallas_call | solution.py:589
  154.6 3.2 %write_out.1 = (f32[256,1024]{1,0:T(8,128)}, f32[256,1024]{1,0:T(8,128)}, f32[256,1024]{1,0:T(8,128)}, f32[256,256]{1,0:T(8,128)}, f32[1024,1024]{1,0:T(8,128)}) custom-call(f32[256,1024]{1,0:T(8,128)S(1)} %get-tuple-element.10.refs_0_, f32[256,1024]{1,0:T(8,128)S(1)} %get-tuple-element.11.refs_1_, f32[256,1024]{1,0:T(8,128)S(1)} %get-tuple-element.12.refs_2_, ...), custom_call_target="tpu_custom_call" | custom-call | tf_op jit(solution)/shard_map/write_out/pallas_call | solution.py:601

commit v6 on v5

--- a/solution.py
+++ b/solution.py
@@ -21,7 +21,7 @@
 NU = 2
 NG = 2
 NDEV = 4
-NSEND = 69
+NSEND = 68
 VMEM_BYTES = 56 * 2**20
 
 ROWS_T = (((0,), (0,)), ((), ()))
@@ -317,7 +317,10 @@
 
     send(lambda: grow.at[opp, head], lambda: gi.at[i, head], lambda: r_gi.at[i, 0], opp, z, z == 2 - y)
 
+    calm = y == z // 2
+    dup = i == z
     send(*gj_part(grow.at[z], 1, False), opp, z)
+    send(*gj_part(grow.at[z], 1, True), opp, z, jnp.logical_not(calm))
     send(lambda: grow.at[z], lambda: gj.at[0], lambda: r_gj.at[0], sib, z)
 
     def gi_send(b, valid):
@@ -326,7 +329,6 @@
             cond = jnp.logical_and(there, jnp.logical_or(b != opp, z == 3 - 3 * y)) if n == 0 else there
             send(lambda: grow.at[b, rows], lambda: gi.at[i, rows], lambda: r_gi.at[i, n], b, z, cond)
 
-    gi_send(z, z >= 0)
     line_last(grow, r_g32, 1)
     gi_send(z - 1, z >= 1)
     gi_send(z + 1, z + 1 < NDEV)
@@ -425,22 +427,29 @@
 
         lax.fori_loop(0, tc // tr, body, 0)
 
-    def gi_arrived(row, n, turned=None):
-        if n == 1:
-            arrived(gi.at[row, gparts[2]], r_gi.at[row, 2], row, z)
-        else:
-            arrived(gi.at[row, gparts[1]], r_gi.at[row, 1], row, z)
-            if row is opp:
-                @pl.when(z == 3 * y)
-                def _():
+    def gi_arrived(row, n, slot, turned=None):
+        @pl.when(jnp.logical_not(dup))
+        def _():
+            if n == 1:
+                arrived(gi.at[row, gparts[2]], r_gi.at[row, 2], row, z)
+            else:
+                arrived(gi.at[row, gparts[1]], r_gi.at[row, 1], row, z)
+                if row is opp:
+                    @pl.when(z == 3 * y)
+                    def _():
+                        arrived(gi.at[row, head], r_gi.at[row, 0], row, z)
+
+                    @pl.when(z == 3 - 3 * y)
+                    def _():
+                        arrived(gi.at[row, head], r_gi.at[row, 0], i, z - ahead)
+                else:
                     arrived(gi.at[row, head], r_gi.at[row, 0], row, z)
-
-                @pl.when(z == 3 - 3 * y)
-                def _():
-                    arrived(gi.at[row, head], r_gi.at[row, 0], i, z - ahead)
-            else:
-                arrived(gi.at[row, head], r_gi.at[row, 0], row, z)
-        gi_split(row, gi.at[row], n)
+            gi_split(row, gi.at[row], n)
+
+        @pl.when(dup)
+        def _():
+            gi_split(row, gj.at[slot], n)
+
         if turned is not None:
             for t in range(3):
                 git[turned, :, pl.ds(t * tr + n * grows, grows)] = gis[row, t, pl.ds(n * grows, grows)].T
@@ -465,7 +474,7 @@
             gi_split(i, grow.at[i], n)
         right_add(i, 0, first=True)
         for n in range(NG):
-            gi_arrived(sib, n)
+            gi_arrived(sib, n, 0)
         right_add(sib, 1)
 
     pl.when(jnp.logical_not(far))(chip_rows)
@@ -473,31 +482,41 @@
     send(*gj_part(gj.at[1], 2, False), sib, z)
     relay(2 - y, i, z - ahead)
     gj_split(2, gj.at[1], 0, early)
+
+    def gj_late_arrived():
+        arrived(gj.at[1, :, pl.ds(early, tc - early)], r_gj.at[3], opp, z)
+
+    pl.when(calm)(gj_late_arrived)
+    send(*gj_part(gj.at[1], 2, True), sib, z, calm)
+
+    @pl.when(calm)
+    def _():
+        gj_split(2, gj.at[1], early, tc - early)
     u_round(1)
     line_last(grow, r_g32, 3)
     gi_send(z - 3, z >= 3)
     gi_send(z + 3, z + 3 < NDEV)
-    send(*gj_part(grow.at[z], 1, True), opp, z, held=late_waits)
+    send(*gj_part(grow.at[z], 1, True), opp, z, calm, held=late_waits)
     arrived(gj.at[2, :, pl.ds(0, early)], r_gj.at[2], sib, z)
     gj_split(3, gj.at[2], 0, early)
+
+    def gj_last_arrived():
+        arrived(gj.at[2, :, pl.ds(early, tc - early)], r_gj.at[4], sib, z)
+        gj_split(3, gj.at[2], early, tc - early)
+
+    pl.when(calm)(gj_last_arrived)
     pl.when(far)(chip_rows)
     u_round(2)
     for n in range(NG - 1):
-        gi_arrived(opp, n, 0)
+        gi_arrived(opp, n, 1, 0)
         right_add(opp, 2, n, 0, early, turned=0)
-        gi_arrived(dia, n, 1)
+        gi_arrived(dia, n, 2, 1)
         right_add(dia, 3, n, 0, early, turned=1)
-
-    @pl.when(inner)
-    def _():
-        arrived(qrx.at[other_half], r_qx.at[1], sib, z)
-        arrived(kx, r_qx.at[2], i, 3 * (z // 2))
-        ubuf[z] += lax.dot_general(kx[...], qrx[...], COLS_T, preferred_element_type=F32)
 
     loads["w"].wait()
     loads["l"].wait()
-    gi_arrived(dia, NG - 1, 1)
-    gi_arrived(opp, NG - 1, 0)
+    gi_arrived(dia, NG - 1, 2, 1)
+    gi_arrived(opp, NG - 1, 1, 0)
 
     left_part(dia, 3)
     send(lambda: lx.at[3], lambda: lrecv.at[2], lambda: r_l.at[2], sib, z)
@@ -509,18 +528,27 @@
     send(lambda: lx.at[2], lambda: lrecv.at[1], lambda: r_l.at[1], opp, z, held=late_waits)
     left_part(i, 0)
     right_add(opp, 2, NG - 1, 0, early, turned=0)
-    arrived(gj.at[1, :, pl.ds(early, tc - early)], r_gj.at[3], opp, z)
-    send(*gj_part(gj.at[1], 2, True), sib, z, held=late_waits)
+    pl.when(jnp.logical_not(calm))(gj_late_arrived)
+    send(*gj_part(gj.at[1], 2, True), sib, z, jnp.logical_not(calm), held=late_waits)
     right_add(dia, 3, NG - 1, 0, early, turned=1)
-    gj_split(2, gj.at[1], early, tc - early)
+
+    @pl.when(jnp.logical_not(calm))
+    def _():
+        gj_split(2, gj.at[1], early, tc - early)
+
     right_add(opp, 2, None, early, tc - early, turned=0)
+
+    @pl.when(inner)
+    def _():
+        arrived(qrx.at[other_half], r_qx.at[1], sib, z)
+        arrived(kx, r_qx.at[2], i, 3 * (z // 2))
+        ubuf[z] += lax.dot_general(kx[...], qrx[...], COLS_T, preferred_element_type=F32)
 
     u_round(3)
     wbuf[...] = wbuf[...] - LR * ubuf[z]
     settle(waits)
     settle(line_waits)
-    arrived(gj.at[2, :, pl.ds(early, tc - early)], r_gj.at[4], sib, z)
-    gj_split(3, gj.at[2], early, tc - early)
+    pl.when(jnp.logical_not(calm))(gj_last_arrived)
     right_add(dia, 3, None, early, tc - early, turned=1)
     arrived(lrecv.at[0], r_l.at[0], sib, z)
     left_sum = lx[0] + lrecv[0]

time: 159 us -> 162 us (1.019)
  the two profiles are of different devices: /device:TPU:0 before, /device:TPU:12 now
where the time goes in v6:
time: 162 us
  Pallas kernels  161 us (99%)
    pallas_call x1, Pallas kernels, local_step(): pl.pallas_call(kernel, name='soap_step', out_shape=[pltpu.VMEM(o.shape, o...  158 us
    pallas_call x1, Pallas kernels, local_step(): pl.pallas_call(write_out, name='write_out', out_shape=[jax.ShapeDtypeStru...  3.24 us

profile of v6, /device:TPU:12, one launch (start us, length us, event | category | flops | bytes accessed | tf_op | source)
XLA Modules:
  0.0 161.6 jit_solution(16359680561367314001)
XLA Ops:
  0.6 157.6 %soap_step.1 = (f32[256,1024]{1,0:T(8,128)S(1)}, f32[256,1024]{1,0:T(8,128)S(1)}, f32[256,1024]{1,0:T(8,128)S(1)}, f32[256,256]{1,0:T(8,128)S(1)}, f32[1024,1024]{1,0:T(8,128)S(1)}) custom-call(f32[256,1024]{1,0:T(8,128)} %w_hbm.1, f32[256,1024]{1,0:T(8,128)} %g_hbm.1, f32[256,1024]{1,0:T(8,128)} %m_hbm.1, f32[256,1024]{1,0:T(8,128)} %v_hbm.1, ...), custom_call_target="tpu_custom_call" | custom-call | tf_op jit(solution)/shard_map/soap_step/pallas_call | solution.py:617
  158.2 3.2 %write_out.1 = (f32[256,1024]{1,0:T(8,128)}, f32[256,1024]{1,0:T(8,128)}, f32[256,1024]{1,0:T(8,128)}, f32[256,256]{1,0:T(8,128)}, f32[1024,1024]{1,0:T(8,128)}) custom-call(f32[256,1024]{1,0:T(8,128)S(1)} %get-tuple-element.10.refs_0_, f32[256,1024]{1,0:T(8,128)S(1)} %get-tuple-element.11.refs_1_, f32[256,1024]{1,0:T(8,128)S(1)} %get-tuple-element.12.refs_2_, ...), custom_call_target="tpu_custom_call" | custom-call | tf_op jit(solution)/shard_map/write_out/pallas_call | solution.py:629

commit v7 on v6

--- a/solution.py
+++ b/solution.py
@@ -486,17 +486,18 @@
     def gj_late_arrived():
         arrived(gj.at[1, :, pl.ds(early, tc - early)], r_gj.at[3], opp, z)
 
-    pl.when(calm)(gj_late_arrived)
-    send(*gj_part(gj.at[1], 2, True), sib, z, calm)
-
-    @pl.when(calm)
-    def _():
-        gj_split(2, gj.at[1], early, tc - early)
     u_round(1)
     line_last(grow, r_g32, 3)
     gi_send(z - 3, z >= 3)
     gi_send(z + 3, z + 3 < NDEV)
     send(*gj_part(grow.at[z], 1, True), opp, z, calm, held=late_waits)
+    pl.when(calm)(gj_late_arrived)
+    send(*gj_part(gj.at[1], 2, True), sib, z, calm)
+
+    @pl.when(calm)
+    def _():
+        gj_split(2, gj.at[1], early, tc - early)
+
     arrived(gj.at[2, :, pl.ds(0, early)], r_gj.at[2], sib, z)
     gj_split(3, gj.at[2], 0, early)
 

time: 162 us -> 157 us (0.969)
  the two profiles are of different devices: /device:TPU:12 before, /device:TPU:0 now
where the time goes in v7:
time: 157 us
  Pallas kernels  156 us (99%)
    pallas_call x1, Pallas kernels, local_step(): pl.pallas_call(kernel, name='soap_step', out_shape=[pltpu.VMEM(o.shape, o...  153 us
    pallas_call x1, Pallas kernels, local_step(): pl.pallas_call(write_out, name='write_out', out_shape=[jax.ShapeDtypeStru...  3.24 us

profile of v7, /device:TPU:0, one launch (start us, length us, event | category | flops | bytes accessed | tf_op | source)
XLA Modules:
  0.0 157.0 jit_solution(5761974605997802650)
XLA Ops:
  0.6 153.0 %soap_step.1 = (f32[256,1024]{1,0:T(8,128)S(1)}, f32[256,1024]{1,0:T(8,128)S(1)}, f32[256,1024]{1,0:T(8,128)S(1)}, f32[256,256]{1,0:T(8,128)S(1)}, f32[1024,1024]{1,0:T(8,128)S(1)}) custom-call(f32[256,1024]{1,0:T(8,128)} %w_hbm.1, f32[256,1024]{1,0:T(8,128)} %g_hbm.1, f32[256,1024]{1,0:T(8,128)} %m_hbm.1, f32[256,1024]{1,0:T(8,128)} %v_hbm.1, ...), custom_call_target="tpu_custom_call" | custom-call | tf_op jit(solution)/shard_map/soap_step/pallas_call | solution.py:618
  153.6 3.2 %write_out.1 = (f32[256,1024]{1,0:T(8,128)}, f32[256,1024]{1,0:T(8,128)}, f32[256,1024]{1,0:T(8,128)}, f32[256,256]{1,0:T(8,128)}, f32[1024,1024]{1,0:T(8,128)}) custom-call(f32[256,1024]{1,0:T(8,128)S(1)} %get-tuple-element.10.refs_0_, f32[256,1024]{1,0:T(8,128)S(1)} %get-tuple-element.11.refs_1_, f32[256,1024]{1,0:T(8,128)S(1)} %get-tuple-element.12.refs_2_, ...), custom_call_target="tpu_custom_call" | custom-call | tf_op jit(solution)/shard_map/write_out/pallas_call | solution.py:630

commit v8 on v7

--- a/solution.py
+++ b/solution.py
@@ -21,7 +21,7 @@
 NU = 2
 NG = 2
 NDEV = 4
-NSEND = 68
+NSEND = 69
 VMEM_BYTES = 56 * 2**20
 
 ROWS_T = (((0,), (0,)), ((), ()))
@@ -407,25 +407,28 @@
         for t, term in enumerate(split3(ref[rows])):
             gis[k, t, rows] = term
 
-    def right_add(k, slot, n=None, start=0, size=None, first=False, turned=None):
+    def right_add(blocks, n=None, start=0, size=None, first=False, unroll=1):
         begin, depth = (0, tr) if n is None else (n * grows, grows)
         cols = pl.ds(start, size or tc)
 
         def body(m, carry):
             rows = pl.ds(pl.multiple_of(m * tr, tr), tr)
-            if turned is None:
-                a0, a1, a2 = [gis[k, t, pl.ds(begin, depth), rows].T for t in range(3)]
-            else:
-                a0, a1, a2 = [git[turned, rows, pl.ds(t * tr + begin, depth)] for t in range(3)]
-            b0, b1, b2 = [qrc[slot, pl.ds(t * tr + begin, depth), cols] for t in range(3)]
-            left = jnp.concatenate([a0, a0, a0, a1, a1, a2], axis=1)
-            right = jnp.concatenate([b0, b1, b2, b0, b1, b0], axis=0)
+            left, right = [], []
+            for k, slot, turned in blocks:
+                if turned is None:
+                    a = [gis[k, t, pl.ds(begin, depth), rows].T for t in range(3)]
+                else:
+                    a = [git[turned, rows, pl.ds(t * tr + begin, depth)] for t in range(3)]
+                b = [qrc[slot, pl.ds(t * tr + begin, depth), cols] for t in range(3)]
+                left += [a[0], a[0], a[0], a[1], a[1], a[2]]
+                right += [b[0], b[1], b[2], b[0], b[1], b[0]]
+            left, right = jnp.concatenate(left, axis=1), jnp.concatenate(right, axis=0)
             share = (1.0 - BETA2) * jnp.dot(left, right, preferred_element_type=F32)
             old = racc[rows, cols]
             racc[rows, cols] = (BETA2 * old if first else old) + share
             return carry
 
-        lax.fori_loop(0, tc // tr, body, 0)
+        lax.fori_loop(0, tc // tr, body, 0, unroll=unroll)
 
     def gi_arrived(row, n, slot, turned=None):
         @pl.when(jnp.logical_not(dup))
@@ -472,10 +475,10 @@
     def chip_rows():
         for n in range(NG):
             gi_split(i, grow.at[i], n)
-        right_add(i, 0, first=True)
+        right_add([(i, 0, None)], first=True)
         for n in range(NG):
             gi_arrived(sib, n, 0)
-        right_add(sib, 1)
+        right_add([(sib, 1, None)])
 
     pl.when(jnp.logical_not(far))(chip_rows)
     arrived(gj.at[1, :, pl.ds(0, early)], r_gj.at[1], opp, z)
@@ -490,7 +493,7 @@
     line_last(grow, r_g32, 3)
     gi_send(z - 3, z >= 3)
     gi_send(z + 3, z + 3 < NDEV)
-    send(*gj_part(grow.at[z], 1, True), opp, z, calm, held=late_waits)
+    send(*gj_part(grow.at[z], 1, True), opp, z, jnp.logical_and(calm, inner), held=late_waits)
     pl.when(calm)(gj_late_arrived)
     send(*gj_part(gj.at[1], 2, True), sib, z, calm)
 
@@ -508,11 +511,13 @@
     pl.when(calm)(gj_last_arrived)
     pl.when(far)(chip_rows)
     u_round(2)
+    others = [(opp, 2, 0), (dia, 3, 1)]
     for n in range(NG - 1):
         gi_arrived(opp, n, 1, 0)
-        right_add(opp, 2, n, 0, early, turned=0)
         gi_arrived(dia, n, 2, 1)
-        right_add(dia, 3, n, 0, early, turned=1)
+        right_add(others, n, 0, early)
+
+    send(*gj_part(grow.at[z], 1, True), opp, z, jnp.logical_and(calm, jnp.logical_not(inner)), held=late_waits)
 
     loads["w"].wait()
     loads["l"].wait()
@@ -522,22 +527,19 @@
     left_part(dia, 3)
     send(lambda: lx.at[3], lambda: lrecv.at[2], lambda: r_l.at[2], sib, z)
     left_part(opp, 2)
-    left_part(sib, 1)
-    send(lambda: lx.at[1], lambda: lrecv.at[0], lambda: r_l.at[0], sib, z)
     arrived(lrecv.at[2], r_l.at[2], sib, z)
     lx[2] += lrecv[2]
     send(lambda: lx.at[2], lambda: lrecv.at[1], lambda: r_l.at[1], opp, z, held=late_waits)
+    left_part(sib, 1)
+    send(lambda: lx.at[1], lambda: lrecv.at[0], lambda: r_l.at[0], sib, z, held=late_waits)
     left_part(i, 0)
-    right_add(opp, 2, NG - 1, 0, early, turned=0)
+    right_add(others, NG - 1, 0, early, unroll=2)
     pl.when(jnp.logical_not(calm))(gj_late_arrived)
     send(*gj_part(gj.at[1], 2, True), sib, z, jnp.logical_not(calm), held=late_waits)
-    right_add(dia, 3, NG - 1, 0, early, turned=1)
 
     @pl.when(jnp.logical_not(calm))
     def _():
         gj_split(2, gj.at[1], early, tc - early)
-
-    right_add(opp, 2, None, early, tc - early, turned=0)
 
     @pl.when(inner)
     def _():
@@ -545,12 +547,12 @@
         arrived(kx, r_qx.at[2], i, 3 * (z // 2))
         ubuf[z] += lax.dot_general(kx[...], qrx[...], COLS_T, preferred_element_type=F32)
 
+    pl.when(jnp.logical_not(calm))(gj_last_arrived)
+    right_add(others, None, early, tc - early, unroll=2)
     u_round(3)
     wbuf[...] = wbuf[...] - LR * ubuf[z]
     settle(waits)
     settle(line_waits)
-    pl.when(jnp.logical_not(calm))(gj_last_arrived)
-    right_add(dia, 3, None, early, tc - early, turned=1)
     arrived(lrecv.at[0], r_l.at[0], sib, z)
     left_sum = lx[0] + lrecv[0]
     arrived(lrecv.at[1], r_l.at[1], opp, z)

time: 157 us -> 158 us (level)
  no operation moved by 1% of the time
where the time goes in v8:
time: 158 us; the launch traced here: 157 us
  Pallas kernels  156 us (99%)
    pallas_call x1, Pallas kernels, local_step(): pl.pallas_call(kernel, name='soap_step', out_shape=[pltpu.VMEM(o.shape, o...  153 us
    pallas_call x1, Pallas kernels, local_step(): pl.pallas_call(write_out, name='write_out', out_shape=[jax.ShapeDtypeStru...  3.24 us

profile of v8, /device:TPU:0, one launch (start us, length us, event | category | flops | bytes accessed | tf_op | source)
XLA Modules:
  0.0 157.1 jit_solution(13200642504187044772)
XLA Ops:
  0.6 153.0 %soap_step.1 = (f32[256,1024]{1,0:T(8,128)S(1)}, f32[256,1024]{1,0:T(8,128)S(1)}, f32[256,1024]{1,0:T(8,128)S(1)}, f32[256,256]{1,0:T(8,128)S(1)}, f32[1024,1024]{1,0:T(8,128)S(1)}) custom-call(f32[256,1024]{1,0:T(8,128)} %w_hbm.1, f32[256,1024]{1,0:T(8,128)} %g_hbm.1, f32[256,1024]{1,0:T(8,128)} %m_hbm.1, f32[256,1024]{1,0:T(8,128)} %v_hbm.1, ...), custom_call_target="tpu_custom_call" | custom-call | tf_op jit(solution)/shard_map/soap_step/pallas_call | solution.py:620
  153.7 3.2 %write_out.1 = (f32[256,1024]{1,0:T(8,128)}, f32[256,1024]{1,0:T(8,128)}, f32[256,1024]{1,0:T(8,128)}, f32[256,256]{1,0:T(8,128)}, f32[1024,1024]{1,0:T(8,128)}) custom-call(f32[256,1024]{1,0:T(8,128)S(1)} %get-tuple-element.10.refs_0_, f32[256,1024]{1,0:T(8,128)S(1)} %get-tuple-element.11.refs_1_, f32[256,1024]{1,0:T(8,128)S(1)} %get-tuple-element.12.refs_2_, ...), custom_call_target="tpu_custom_call" | custom-call | tf_op jit(solution)/shard_map/write_out/pallas_call | solution.py:632

commit v9 on v8

--- a/solution.py
+++ b/solution.py
@@ -21,7 +21,7 @@
 NU = 2
 NG = 2
 NDEV = 4
-NSEND = 69
+NSEND = 64
 VMEM_BYTES = 56 * 2**20
 
 ROWS_T = (((0,), (0,)), ((), ()))
@@ -55,11 +55,11 @@
     hcols = tc // NH
     urows = tr // NU
     grows = tr // NG
-    head_rows = 3 * grows // 4
+    head_rows = 5 * grows // 8
     gparts = (pl.ds(0, head_rows), pl.ds(head_rows, grows - head_rows), pl.ds(grows, grows))
     early = tc - tc // 4
 
-    waits, qr_waits, late_waits, line_waits = [], [], [], []
+    waits, qr_waits, late_waits, line_waits, far_waits = [], [], [], [], []
     unused, most = list(range(NSEND)), [0]
 
     def dev(row, col):
@@ -323,11 +323,11 @@
     send(*gj_part(grow.at[z], 1, True), opp, z, jnp.logical_not(calm))
     send(lambda: grow.at[z], lambda: gj.at[0], lambda: r_gj.at[0], sib, z)
 
-    def gi_send(b, valid):
+    def gi_send(b, valid, held=None):
         there = jnp.logical_and(valid, b != i)
         for n, rows in enumerate(gparts):
             cond = jnp.logical_and(there, jnp.logical_or(b != opp, z == 3 - 3 * y)) if n == 0 else there
-            send(lambda: grow.at[b, rows], lambda: gi.at[i, rows], lambda: r_gi.at[i, n], b, z, cond)
+            send(lambda: grow.at[b, rows], lambda: gi.at[i, rows], lambda: r_gi.at[i, n], b, z, cond, held)
 
     line_last(grow, r_g32, 1)
     gi_send(z - 1, z >= 1)
@@ -491,8 +491,8 @@
 
     u_round(1)
     line_last(grow, r_g32, 3)
-    gi_send(z - 3, z >= 3)
-    gi_send(z + 3, z + 3 < NDEV)
+    gi_send(z - 3, z >= 3, far_waits)
+    gi_send(z + 3, z + 3 < NDEV, far_waits)
     send(*gj_part(grow.at[z], 1, True), opp, z, jnp.logical_and(calm, inner), held=late_waits)
     pl.when(calm)(gj_late_arrived)
     send(*gj_part(gj.at[1], 2, True), sib, z, calm)
@@ -517,17 +517,17 @@
         gi_arrived(dia, n, 2, 1)
         right_add(others, n, 0, early)
 
-    send(*gj_part(grow.at[z], 1, True), opp, z, jnp.logical_and(calm, jnp.logical_not(inner)), held=late_waits)
-
     loads["w"].wait()
     loads["l"].wait()
     gi_arrived(dia, NG - 1, 2, 1)
     gi_arrived(opp, NG - 1, 1, 0)
 
     left_part(dia, 3)
+    settle(far_waits)
     send(lambda: lx.at[3], lambda: lrecv.at[2], lambda: r_l.at[2], sib, z)
     left_part(opp, 2)
     arrived(lrecv.at[2], r_l.at[2], sib, z)
+    send(*gj_part(grow.at[z], 1, True), opp, z, jnp.logical_and(calm, jnp.logical_not(inner)), held=late_waits)
     lx[2] += lrecv[2]
     send(lambda: lx.at[2], lambda: lrecv.at[1], lambda: r_l.at[1], opp, z, held=late_waits)
     left_part(sib, 1)

time: 158 us -> 153 us (0.968)
  Pallas kernels: 156 us -> 151 us
    pallas_call x1, Pallas kernels: 153 us -> 148 us  [local_step(): pl.pallas_call(kernel, name='soap_step', out_shape=[pltpu.VMEM(o.shape, o...]
where the time goes in v9:
time: 153 us; the launch traced here: 152 us
  Pallas kernels  151 us (99%)
    pallas_call x1, Pallas kernels, local_step(): pl.pallas_call(kernel, name='soap_step', out_shape=[pltpu.VMEM(o.shape, o...  148 us
    pallas_call x1, Pallas kernels, local_step(): pl.pallas_call(write_out, name='write_out', out_shape=[jax.ShapeDtypeStru...  3.24 us

profile of v9, /device:TPU:0, one launch (start us, length us, event | category | flops | bytes accessed | tf_op | source)
XLA Modules:
  0.0 152.1 jit_solution(13415789533217259442)
XLA Ops:
  0.6 148.1 %soap_step.1 = (f32[256,1024]{1,0:T(8,128)S(1)}, f32[256,1024]{1,0:T(8,128)S(1)}, f32[256,1024]{1,0:T(8,128)S(1)}, f32[256,256]{1,0:T(8,128)S(1)}, f32[1024,1024]{1,0:T(8,128)S(1)}) custom-call(f32[256,1024]{1,0:T(8,128)} %w_hbm.1, f32[256,1024]{1,0:T(8,128)} %g_hbm.1, f32[256,1024]{1,0:T(8,128)} %m_hbm.1, f32[256,1024]{1,0:T(8,128)} %v_hbm.1, ...), custom_call_target="tpu_custom_call" | custom-call | tf_op jit(solution)/shard_map/soap_step/pallas_call | solution.py:620
  148.7 3.2 %write_out.1 = (f32[256,1024]{1,0:T(8,128)}, f32[256,1024]{1,0:T(8,128)}, f32[256,1024]{1,0:T(8,128)}, f32[256,256]{1,0:T(8,128)}, f32[1024,1024]{1,0:T(8,128)}) custom-call(f32[256,1024]{1,0:T(8,128)S(1)} %get-tuple-element.10.refs_0_, f32[256,1024]{1,0:T(8,128)S(1)} %get-tuple-element.11.refs_1_, f32[256,1024]{1,0:T(8,128)S(1)} %get-tuple-element.12.refs_2_, ...), custom_call_target="tpu_custom_call" | custom-call | tf_op jit(solution)/shard_map/write_out/pallas_call | solution.py:632

commit v10 on v9

--- a/solution.py
+++ b/solution.py
@@ -55,7 +55,7 @@
     hcols = tc // NH
     urows = tr // NU
     grows = tr // NG
-    head_rows = 5 * grows // 8
+    head_rows = 3 * grows // 4
     gparts = (pl.ds(0, head_rows), pl.ds(head_rows, grows - head_rows), pl.ds(grows, grows))
     early = tc - tc // 4
 
@@ -481,15 +481,15 @@
         right_add([(sib, 1, None)])
 
     pl.when(jnp.logical_not(far))(chip_rows)
+    relay(2 - y, i, z - ahead)
+    u_round(1)
     arrived(gj.at[1, :, pl.ds(0, early)], r_gj.at[1], opp, z)
     send(*gj_part(gj.at[1], 2, False), sib, z)
-    relay(2 - y, i, z - ahead)
     gj_split(2, gj.at[1], 0, early)
 
     def gj_late_arrived():
         arrived(gj.at[1, :, pl.ds(early, tc - early)], r_gj.at[3], opp, z)
 
-    u_round(1)
     line_last(grow, r_g32, 3)
     gi_send(z - 3, z >= 3, far_waits)
     gi_send(z + 3, z + 3 < NDEV, far_waits)
@@ -533,7 +533,7 @@
     left_part(sib, 1)
     send(lambda: lx.at[1], lambda: lrecv.at[0], lambda: r_l.at[0], sib, z, held=late_waits)
     left_part(i, 0)
-    right_add(others, NG - 1, 0, early, unroll=2)
+    right_add(others, NG - 1, 0, early)
     pl.when(jnp.logical_not(calm))(gj_late_arrived)
     send(*gj_part(gj.at[1], 2, True), sib, z, jnp.logical_not(calm), held=late_waits)
 

time: 153 us -> 153 us (level)
  no operation moved by 1% of the time
where the time goes in v10:
time: 153 us; the launch traced here: 151 us
  Pallas kernels  151 us (99%)
    pallas_call x1, Pallas kernels, local_step(): pl.pallas_call(kernel, name='soap_step', out_shape=[pltpu.VMEM(o.shape, o...  147 us
    pallas_call x1, Pallas kernels, local_step(): pl.pallas_call(write_out, name='write_out', out_shape=[jax.ShapeDtypeStru...  3.24 us

profile of v10, /device:TPU:0, one launch (start us, length us, event | category | flops | bytes accessed | tf_op | source)
XLA Modules:
  0.0 151.4 jit_solution(3588624113849979762)
XLA Ops:
  0.6 147.4 %soap_step.1 = (f32[256,1024]{1,0:T(8,128)S(1)}, f32[256,1024]{1,0:T(8,128)S(1)}, f32[256,1024]{1,0:T(8,128)S(1)}, f32[256,256]{1,0:T(8,128)S(1)}, f32[1024,1024]{1,0:T(8,128)S(1)}) custom-call(f32[256,1024]{1,0:T(8,128)} %w_hbm.1, f32[256,1024]{1,0:T(8,128)} %g_hbm.1, f32[256,1024]{1,0:T(8,128)} %m_hbm.1, f32[256,1024]{1,0:T(8,128)} %v_hbm.1, ...), custom_call_target="tpu_custom_call" | custom-call | tf_op jit(solution)/shard_map/soap_step/pallas_call | solution.py:620
  148.0 3.2 %write_out.1 = (f32[256,1024]{1,0:T(8,128)}, f32[256,1024]{1,0:T(8,128)}, f32[256,1024]{1,0:T(8,128)}, f32[256,256]{1,0:T(8,128)}, f32[1024,1024]{1,0:T(8,128)}) custom-call(f32[256,1024]{1,0:T(8,128)S(1)} %get-tuple-element.10.refs_0_, f32[256,1024]{1,0:T(8,128)S(1)} %get-tuple-element.11.refs_1_, f32[256,1024]{1,0:T(8,128)S(1)} %get-tuple-element.12.refs_2_, ...), custom_call_target="tpu_custom_call" | custom-call | tf_op jit(solution)/shard_map/write_out/pallas_call | solution.py:632

commit v11 on v10

--- a/solution.py
+++ b/solution.py
@@ -460,10 +460,11 @@
     def left_part(k, slot):
         pieces = [gis[k, t] for t in range(3)]
         other = [gis[z, t] for t in range(3)]
-        total = None
-        for t, u in ((0, 0), (0, 1), (1, 0), (1, 1), (0, 2), (2, 0)):
-            d = lax.dot_general(pieces[t], other[u], COLS_T, preferred_element_type=F32)
-            total = d if total is None else total + d
+        d0, d1, d2 = [
+            lax.dot_general(jnp.concatenate(pieces[:3 - u], axis=0), other[u], COLS_T, preferred_element_type=F32)
+            for u in range(3)
+        ]
+        total = ((d0[:tr] + d0[tr:2 * tr]) + (d1[:tr] + d1[tr:])) + (d0[2 * tr:] + d2)
         lx[slot] = total
 
     settle(qr_waits)

time: 153 us -> 153 us (level)
  no operation moved by 1% of the time
where the time goes in v11:
time: 153 us; the launch traced here: 151 us
  Pallas kernels  151 us (99%)
    pallas_call x1, Pallas kernels, local_step(): pl.pallas_call(kernel, name='soap_step', out_shape=[pltpu.VMEM(o.shape, o...  147 us
    pallas_call x1, Pallas kernels, local_step(): pl.pallas_call(write_out, name='write_out', out_shape=[jax.ShapeDtypeStru...  3.24 us

profile of v11, /device:TPU:0, one launch (start us, length us, event | category | flops | bytes accessed | tf_op | source)
XLA Modules:
  0.0 151.4 jit_solution(14222561283090221972)
XLA Ops:
  0.6 147.4 %soap_step.1 = (f32[256,1024]{1,0:T(8,128)S(1)}, f32[256,1024]{1,0:T(8,128)S(1)}, f32[256,1024]{1,0:T(8,128)S(1)}, f32[256,256]{1,0:T(8,128)S(1)}, f32[1024,1024]{1,0:T(8,128)S(1)}) custom-call(f32[256,1024]{1,0:T(8,128)} %w_hbm.1, f32[256,1024]{1,0:T(8,128)} %g_hbm.1, f32[256,1024]{1,0:T(8,128)} %m_hbm.1, f32[256,1024]{1,0:T(8,128)} %v_hbm.1, ...), custom_call_target="tpu_custom_call" | custom-call | tf_op jit(solution)/shard_map/soap_step/pallas_call | solution.py:621
  148.0 3.2 %write_out.1 = (f32[256,1024]{1,0:T(8,128)}, f32[256,1024]{1,0:T(8,128)}, f32[256,1024]{1,0:T(8,128)}, f32[256,256]{1,0:T(8,128)}, f32[1024,1024]{1,0:T(8,128)}) custom-call(f32[256,1024]{1,0:T(8,128)S(1)} %get-tuple-element.10.refs_0_, f32[256,1024]{1,0:T(8,128)S(1)} %get-tuple-element.11.refs_1_, f32[256,1024]{1,0:T(8,128)S(1)} %get-tuple-element.12.refs_2_, ...), custom_call_target="tpu_custom_call" | custom-call | tf_op jit(solution)/shard_map/write_out/pallas_call | solution.py:633
